TPU v7x, 128 devices: a whole 4x4x4 slice. The times are simulated.
128 devices in a mesh: day: 16 (over x, y), pair: 8 (over z, core).
Axes of the slice: x: 4, y: 4, z: 4, core: 2. Of those that a mesh axis runs over, the one named last changes fastest.
Arguments:
- correlations: bfloat16 [64, 4096, 2001], P('day', 'pair'), may hold values from -8 to 8
- mask: int32 [64, 4096], P('day', 'pair'), may hold values from 0 to 1, as said below
- counts: int32 [4096], P(('pair', 'day')), may hold values from 1 to 64, as said below
Outputs:
- phase_weighted: float32 [4096, 2001], P(('pair', 'day'))
- linear: float32 [4096, 2001], P(('pair', 'day'))
Inputs may be any that keep to these rules, and one draw needn't show every extreme that they name: `mask`: every pair has a usable correlation on at least one day. counts[p] equals the number of days d with mask[d, p] = 1.
All inputs are finite; a program needn't handle non-finite values.
Results may differ from a plain program's by a relative error of at most 0.00044.
Values may be sent and summed in bfloat16 or wider, within the bound.
No kernel may reach another device: no remote copies, remote signals or barrier semaphores. Data moves between devices by JAX's collectives and lax.ppermute only.
A program may use at most 128 MiB of HBM per device.

v0:
```python
import jax
import jax.numpy as jnp
from jax import lax
from jax.sharding import PartitionSpec as P


def copy_for_each(x, axis):
    count = lax.axis_size(axis)
    return lax.all_to_all(jnp.broadcast_to(x[None], (count, *x.shape)), axis, 0, 0, tiled=True)


def of_everyone(x, axis):
    everything = copy_for_each(x, axis)
    return jnp.sum(everything, axis=0)


def together(arrays, axis):
    line, at, finished = (jnp.concatenate([a.reshape(-1) for a in arrays]), 0, [])
    total = of_everyone(line, axis)
    for a in arrays:
        finished.append(total[at : at + a.size].reshape(a.shape))
        at += a.size
    return tuple(finished)


def in_order(tiles, dim):
    lengths = list(tiles.shape[1:])
    lengths[dim] *= tiles.shape[0]
    return jnp.moveaxis(tiles, 0, dim).reshape(lengths)


def collect(x, axis, dim):
    return in_order(copy_for_each(x, axis), dim)


def hilbert_table(lag_count):
    row_index = lax.broadcasted_iota(jnp.int32, (lag_count, lag_count), 0)
    col_index = lax.broadcasted_iota(jnp.int32, (lag_count, lag_count), 1)
    offset = (col_index - row_index) % lag_count
    offset = jnp.where(offset > lag_count // 2, offset - lag_count, offset)
    phase_angle = jnp.pi * offset.astype(jnp.float32) / lag_count
    parity = 1.0 - 2.0 * (offset % 2).astype(jnp.float32)
    sine_safe = jnp.where(offset == 0, 1.0, jnp.sin(phase_angle))
    table = jnp.where(offset == 0, 0.0, (jnp.cos(phase_angle) - parity) / (lag_count * sine_safe))
    return table.astype(jnp.bfloat16)


def stack_terms(pieces, weight, kernel_table):
    day_count, pair_count, lag_count = pieces.shape
    flattened = pieces.reshape(day_count * pair_count, lag_count)
    hilbert = jnp.dot(flattened, kernel_table, preferred_element_type=jnp.float32)
    day_scale = weight[:, None, None]
    real_part = day_scale * pieces.astype(jnp.float32)
    imag_part = day_scale * hilbert.reshape(day_count, pair_count, lag_count)
    inverse = lax.rsqrt(real_part * real_part + imag_part * imag_part + 0.25)
    return (
        jnp.sum(real_part, axis=0),
        jnp.sum(real_part * inverse, axis=0),
        jnp.sum(imag_part * inverse, axis=0),
    )


def shards(correlations, mask, counts):
    masked = correlations * mask[:, :, None].astype(jnp.bfloat16)
    energy = jnp.sum(jnp.square(masked.astype(jnp.float32)), axis=(1, 2))
    used_pairs = jnp.sum(mask, axis=1).astype(jnp.float32)
    energy, used_pairs = together((energy, used_pairs), "pair")
    lag_count = correlations.shape[2]
    weight = lax.rsqrt(energy / (lag_count * jnp.maximum(used_pairs, 1.0)) + 0.1)
    kernel_table = hilbert_table(lag_count)
    groups = lax.axis_size("day")
    owned_rows = correlations.shape[1] // groups
    weights_all = collect(weight, "day", 0)
    blocks = masked.reshape(correlations.shape[0], groups, owned_rows, lag_count)
    linear_sum, phase_real, phase_imag = stack_terms(
        lax.all_to_all(blocks, "day", split_axis=1, concat_axis=0, tiled=True)[:, 0],
        weights_all,
        kernel_table,
    )
    divisor = jnp.maximum(counts.astype(jnp.float32), 1.0)[:, None]
    linear = linear_sum / divisor
    coherence = (phase_real * phase_real + phase_imag * phase_imag) / (divisor * divisor)
    return (linear * coherence, linear)


def solution(mesh):
    placed = (P("day", "pair", None), P("day", "pair"), P(("pair", "day")))
    return jax.shard_map(
        shards,
        mesh=mesh,
        in_specs=placed,
        out_specs=(P(("pair", "day"), None), P(("pair", "day"), None)),
        check_vma=False,
    )
```

profile of v0, /device:TPU:28, one launch (start us, length us, event | category | flops | bytes accessed | tf_op | source)
XLA Modules:
  0.0 233.0 jit_solution(9688433474302730955)
XLA Ops:
  0.6 0.9 fusion.38
  1.5 13.7 %copy.19 = bf16[4,512,2001]{2,1,0:T(8,128)(2,1)} copy(bf16[4,512,2001]{1,0,2:T(4,128)(2,1)} %param.3) | data formatting | bytes 16392192 | tf_op args[0]
  15.3 8.3 %multiply_reduce_fusion.3 = (f32[4]{0:T(128)S(1)}, bf16[4,512,2001]{2,1,0:T(8,128)(2,1)}) fusion(bf16[4,512,2001]{2,1,0:T(8,128)(2,1)} %copy.19, bf16[4,512]{1,0:T(4,128)(2,1)S(1)} %get-tuple-element.9), kind=kLoop, calls=%fused_computation.10 | loop fusion | flops 16392188 | bytes 16396304 | tf_op jit(solution)/shard_map/reduce_sum | solution.py:65
  23.6 0.1 pad_maximum_fusion
  23.7 10.4 %all_to_all.27 = f32[8,1,8]{2,1,0:T(1,128)S(1)} all-to-all(f32[8,1,8]{2,1,0:T(1,128)S(1)} %broadcast_in_dim.9), channel_id=1, replica_groups=mesh['day'=16,'pair'=8] {'pair'}, dimensions={0} | all-to-all | bytes 512 | tf_op jit(solution)/shard_map/all_to_all | solution.py:9
  34.1 0.1 add_rsqrt_fusion.1
  34.2 0.6 broadcast_in_dim.10
  34.8 7.1 %all-to-all-start.1 = ((f32[16,1,4]{2,1,0:T(1,128)}), f32[16,1,4]{2,1,0:T(1,128)S(1)}, u32[]{:S(2)}, u32[]{:S(2)}) async-start(f32[16,1,4]{2,1,0:T(1,128)} %broadcast_in_dim.10), calls=%async_computation.1 | async-start | bytes 16384 | tf_op jit(solution)/shard_map/all_to_all | solution.py:9
  41.9 8.3 %copy.23 = bf16[4,16,32,2001]{3,2,0,1:T(8,128)(2,1)} copy(bf16[4,16,32,2001]{3,2,1,0:T(8,128)(2,1)} %bitcast.23) | data formatting | bytes 16392192 | tf_op jit(solution)/shard_map/reshape | solution.py:74
  50.2 0.0 copy-start
  50.2 0.0 all-to-all-done.1
  50.2 7.4 %all-to-all-start.2 = ((bf16[4,16,32,2001]{3,2,0,1:T(8,128)(2,1)}), bf16[4,16,32,2001]{3,2,0,1:T(8,128)(2,1)}, u32[]{:S(2)}, u32[]{:S(2)}) async-start(bf16[4,16,32,2001]{3,2,0,1:T(8,128)(2,1)} %copy.23), calls=%async_computation.2 | async-start | bytes 16777216 | tf_op jit(solution)/shard_map/all_to_all | solution.py:76
  57.5 0.0 copy-done
  57.6 82.2 %fusion.14.clone.4 = bf16[2001,2001,1]{1,0,2:T(8,128)(2,1)} fusion(), kind=kLoop, calls=%fused_computation.24.clone.clone.clone.clone.1 | loop fusion | flops 132132008 | bytes 8008002 | tf_op jit(solution)/shard_map/reduce_sum | solution.py:58
  139.8 0.5 broadcast.52
  140.3 0.7 reduce.5
  141.0 0.1 mul.76
  141.1 60.0 %all-to-all-done.2 = bf16[4,16,32,2001]{3,2,0,1:T(8,128)(2,1)} async-done(((bf16[4,16,32,2001]{3,2,0,1:T(8,128)(2,1)}), bf16[4,16,32,2001]{3,2,0,1:T(8,128)(2,1)}, u32[]{:S(2)}, u32[]{:S(2)}) %all-to-all-start.2) | async-done | bytes 8196128 | tf_op jit(solution)/shard_map/all_to_all | solution.py:76
  201.1 0.0 copy-start.1
  201.1 5.8 %multiply_reduce_fusion.2 = f32[32,2001]{1,0:T(8,128)S(1)} fusion(bf16[4,16,32,2001]{3,2,0,1:T(8,128)(2,1)} %all-to-all-done.2, f32[16,4]{1,0:T(8,128)S(1)} %bitcast.24), kind=kLoop, calls=%fused_computation.9 | loop fusion | flops 12230112 | bytes 8452480 | tf_op jit(solution)/shard_map/reduce_sum | solution.py:57
  206.9 0.0 copy-done.1
  206.9 25.2 %multiply_reduce_fusion.1 = (f32[32,2001]{1,0:T(8,128)S(1)}, f32[32,2001]{1,0:T(8,128)S(1)}) fusion(f32[64]{0:T(128)S(1)} %mul.76, bf16[4,16,32,2001]{3,2,0,1:T(8,128)(2,1)} %all-to-all-done.2, bf16[64,32,2001]{2,1,0:T(8,128)(2,1)} %bitcast.6, bf16[2001,2001,1]{1,0,2:T(8,128)(2,1)S(1)} %copy-done.1), kind=kOutput, calls=%fused_computation.6 | convolution fusion | flops 16445337600 | bytes 24912706 | tf_op jit(solution)/shard_map/dot_general | solution.py:51
  232.1 0.9 divide_multiply_fusion
  (4 shorter events, 0.0 us)
Async XLA Ops:
  34.8 15.4 %all-to-all-start.1 = ((f32[16,1,4]{2,1,0:T(1,128)}), f32[16,1,4]{2,1,0:T(1,128)S(1)}, u32[]{:S(2)}, u32[]{:S(2)}) async-start(f32[16,1,4]{2,1,0:T(1,128)} %broadcast_in_dim.10), calls=%async_computation.1 | async-start | bytes 16384 | tf_op jit(solution)/shard_map/all_to_all | solution.py:9
  50.2 7.4 %copy-start = (s32[32]{0:T(128)S(1)}, s32[32]{0:T(128)}, u32[]{:S(2)}) copy-start(s32[32]{0:T(128)} %param.5) | copy-start | bytes 388
  50.2 150.9 %all-to-all-start.2 = ((bf16[4,16,32,2001]{3,2,0,1:T(8,128)(2,1)}), bf16[4,16,32,2001]{3,2,0,1:T(8,128)(2,1)}, u32[]{:S(2)}, u32[]{:S(2)}) async-start(bf16[4,16,32,2001]{3,2,0,1:T(8,128)(2,1)} %copy.23), calls=%async_computation.2 | async-start | bytes 16777216 | tf_op jit(solution)/shard_map/all_to_all | solution.py:76
  201.1 5.9 %copy-start.1 = (bf16[2001,2001,1]{1,0,2:T(8,128)(2,1)S(1)}, bf16[2001,2001,1]{1,0,2:T(8,128)(2,1)}, u32[]{:S(2)}) copy-start(bf16[2001,2001,1]{1,0,2:T(8,128)(2,1)} %fusion.14.clone.4) | copy-start | bytes 24024010
where the time goes:
time: 234 us; the launch traced here: 233 us
  other arithmetic  99.1 us (42%)
  waiting for transfers between devices  60 us (26%)
  matrix products  25.2 us (11%)
  local copies, waits for them, and re-layouts  23.2 us (10%)
  starting transfers between devices  14.5 us (6%)
  blocking collectives  10.4 us (4%)
    reduce_sum x1, other arithmetic, stack_terms(): jnp.sum(real_part * inverse, axis=0)  82.2 us
    all_to_all x1, waiting for transfers between devices, shards(): lax.all_to_all(blocks, 'day', split_axis=1, concat_axis=0, tiled=True)[:, 0]  60 us
    dot_general x1, matrix products, stack_terms(): jnp.dot(flattened, kernel_table, preferred_element_type=jnp.float32)  25.2 us
    unnamed x5, local copies, waits for them, and re-layouts  13.8 us
    all_to_all x1, blocking collectives, copy_for_each(): lax.all_to_all(jnp.broadcast_to(x[None], (count, *x.shape)), axis, 0, 0,...  10.4 us
    reduce_sum x1, other arithmetic, shards(): energy = jnp.sum(jnp.square(masked.astype(jnp.float32)), axis=(1, 2))  8.34 us
    reshape x1, local copies, waits for them, and re-layouts, shards(): masked.reshape(correlations.shape[0], groups, owned_rows, lag_count)  8.25 us
    all_to_all x1, starting transfers between devices, shards(): lax.all_to_all(blocks, 'day', split_axis=1, concat_axis=0, tiled=True)[:, 0]  7.36 us
  transfers between devices with their start and end apart: 2, of which 1 were waited for; matrix products, arithmetic and copies ran while one was open for 39% of the time, Pallas kernels for 0%

commit v1 on v0

v1 whole, which is shorter than its diff:
```python
import functools

import jax
import jax.numpy as jnp
from jax import lax
from jax.experimental import pallas as pl
from jax.experimental.pallas import tpu as pltpu
from jax.sharding import PartitionSpec as P


LAGS = 2001
WIDTH = 2048
WORDS = WIDTH // 2
OWNED = 32
DAYS = 4
SIDE = 4
QUANTITIES = 3
TOP = 32766.0
KERNEL_SUM = 6.0
MB = 1 << 20

params = functools.partial(pltpu.CompilerParams, vmem_limit_bytes=40 * MB)


def encode(value, scale):
    root = value * lax.rsqrt(jnp.abs(value) + 1e-36)
    return (root * scale + 32768.5).astype(jnp.int32)


def pack(low, high):
    return low | (high << 16)


def unpack(word):
    low = (word & 0xFFFF).astype(jnp.float32) - 32768.0
    high = (lax.shift_right_logical(word, 16)).astype(jnp.float32) - 32768.0
    return low * jnp.abs(low), high * jnp.abs(high)


def unit(exponent):
    return jnp.exp2(exponent.astype(jnp.float32)) * (1.0 / (TOP * TOP))


def table_kernel(ext_ref, out_ref, rolled_ref):
    for q in range(16):
        first = pltpu.roll(ext_ref[...], 16 * q, 1)
        second = pltpu.roll(ext_ref[...], 16 * q + 8, 1)
        rolled_ref[16 * q : 16 * q + 16, :] = jnp.concatenate([first, second], 0).astype(jnp.bfloat16)
    for q in range(8):
        for n in range(8):
            for h in range(2):
                start = 128 * (n + 8 * h) - 256 * q + WIDTH
                out_ref[256 * q : 256 * q + 256, 256 * n + 128 * h : 256 * n + 128 * h + 128] = rolled_ref[
                    :, start : start + 128
                ]


def kernel_table():
    row = lax.broadcasted_iota(jnp.int32, (8, 2 * WIDTH), 0)
    col = lax.broadcasted_iota(jnp.int32, (8, 2 * WIDTH), 1)
    offset = (col - row - WIDTH + 2 * LAGS) % LAGS
    offset = jnp.where(offset > LAGS // 2, offset - LAGS, offset)
    angle = jnp.pi * offset.astype(jnp.float32) / LAGS
    parity = 1.0 - 2.0 * (offset % 2).astype(jnp.float32)
    sine = jnp.where(offset == 0, 1.0, jnp.sin(angle))
    ext = jnp.where(offset == 0, 0.0, (jnp.cos(angle) - parity) / (LAGS * sine))
    ext = ext.astype(jnp.bfloat16).astype(jnp.float32)
    return pl.pallas_call(
        table_kernel,
        out_shape=jax.ShapeDtypeStruct((WIDTH, WIDTH), jnp.bfloat16),
        scratch_shapes=[pltpu.VMEM((256, 2 * WIDTH), jnp.bfloat16)],
        compiler_params=params(),
        name="table",
    )(ext)


def terms_kernel(order_ref, weight_ref, scale_ref, exp_ref, *refs):
    x_refs, (table_ref, out_ref, rows_ref) = refs[:SIDE], refs[SIDE:]
    n = pl.program_id(0)

    @pl.when(n == 0)
    def _():
        lane = lax.broadcasted_iota(jnp.int32, (OWNED, 128), 1)
        for l in range(SIDE):
            for d in range(DAYS):
                at = (l * DAYS + d) * OWNED
                rows_ref[at : at + OWNED, : WIDTH - 128] = x_refs[l][d, :, : WIDTH - 128]
                tail = x_refs[l][d, :, WIDTH - 128 :]
                keep = lane < LAGS - (WIDTH - 128)
                rows_ref[at : at + OWNED, WIDTH - 128 :] = jnp.where(
                    keep, tail.astype(jnp.float32), 0.0
                ).astype(jnp.bfloat16)

    hilbert = jnp.dot(rows_ref[...], table_ref[...], preferred_element_type=jnp.float32)
    for l in range(SIDE):
        codes = []
        for h in range(2):
            lanes = pl.ds(pl.multiple_of(n * 128 + h * WORDS, 128), 128)
            linear = real = imag = None
            for d in range(DAYS):
                at = (l * DAYS + d) * OWNED
                w = weight_ref[d]
                real_part = rows_ref[at : at + OWNED, lanes].astype(jnp.float32) * w
                imag_part = hilbert[at : at + OWNED, 128 * h : 128 * h + 128] * w
                inverse = lax.rsqrt(real_part * real_part + imag_part * imag_part + 0.25)
                a, b = real_part * inverse, imag_part * inverse
                linear = real_part if d == 0 else linear + real_part
                real = a if d == 0 else real + a
                imag = b if d == 0 else imag + b
            codes.append([encode(v, scale_ref[q]) for q, v in enumerate((linear, real, imag))])
        for q in range(QUANTITIES):
            at = (l * QUANTITIES + q) * OWNED
            out_ref[at : at + OWNED, :] = pack(codes[0][q], codes[1][q])
    row = lax.broadcasted_iota(jnp.int32, (8, 128), 0)
    out_ref[SIDE * QUANTITIES * OWNED :, :] = jnp.where(
        row == 0, exp_ref[0], jnp.where(row == 1, exp_ref[1], exp_ref[2])
    )


def terms(k, order, weight, scale, exponent, masked, table):
    rows = SIDE * QUANTITIES * OWNED + 8
    smem = pl.BlockSpec(memory_space=pltpu.SMEM)

    def block(l):
        return pl.BlockSpec((DAYS, OWNED, WIDTH), lambda n, order: (0, order[4 * k + l], 0))

    return pl.pallas_call(
        terms_kernel,
        grid_spec=pltpu.PrefetchScalarGridSpec(
            num_scalar_prefetch=1,
            grid=(8,),
            in_specs=[smem, smem, smem]
            + [block(l) for l in range(SIDE)]
            + [pl.BlockSpec((WIDTH, 256), lambda n, order: (0, n))],
            out_specs=pl.BlockSpec((rows, 128), lambda n, order: (0, n)),
            scratch_shapes=[pltpu.VMEM((SIDE * DAYS * OWNED, WIDTH), jnp.bfloat16)],
        ),
        out_shape=jax.ShapeDtypeStruct((rows, WORDS), jnp.int32),
        compiler_params=params(dimension_semantics=("arbitrary",)),
        cost_estimate=pl.CostEstimate(
            flops=2 * SIDE * DAYS * OWNED * WIDTH * WIDTH, bytes_accessed=12 * MB, transcendentals=0
        ),
        name="terms",
    )(order, weight, scale, exponent, *([masked] * SIDE), table)


def read_sum(body_refs, exp_refs, q, cols):
    low = high = None
    for body, exp in zip(body_refs, exp_refs):
        k = unit(exp[q : q + 1, :])
        a, b = unpack(body[q * OWNED : (q + 1) * OWNED, cols])
        low = a * k if low is None else low + a * k
        high = b * k if high is None else high + b * k
    return low, high


def combine_kernel(*refs):
    body_refs, exp_refs, out_ref = refs[:SIDE], refs[SIDE : 2 * SIDE], refs[2 * SIDE]
    top = exp_refs[0][...]
    for exp in exp_refs[1:]:
        top = jnp.maximum(top, exp[...])
    top = top + 2
    scale = jnp.exp2(-0.5 * top.astype(jnp.float32)) * TOP
    for j in range(WORDS // 128):
        cols = slice(128 * j, 128 * j + 128)
        for q in range(QUANTITIES):
            low, high = read_sum(body_refs, exp_refs, q, cols)
            s = scale[q : q + 1, :]
            out_ref[q * OWNED : (q + 1) * OWNED, cols] = pack(encode(low, s), encode(high, s))
        out_ref[QUANTITIES * OWNED :, cols] = top


def combine(l, messages):
    body = pl.BlockSpec((QUANTITIES * OWNED, WORDS), lambda i: (l, 0))
    exps = pl.BlockSpec((8, 128), lambda i: (SIDE * QUANTITIES * OWNED // 8, 0))
    rows = QUANTITIES * OWNED + 8
    return pl.pallas_call(
        combine_kernel,
        grid=(1,),
        in_specs=[body] * SIDE + [exps] * SIDE,
        out_specs=pl.BlockSpec((rows, WORDS), lambda i: (0, 0)),
        out_shape=jax.ShapeDtypeStruct((rows, WORDS), jnp.int32),
        compiler_params=params(),
        cost_estimate=pl.CostEstimate(flops=2 * MB, bytes_accessed=2 * MB, transcendentals=0),
        name="combine",
    )(*messages, *messages)


def finish_kernel(divisor_ref, *refs):
    body_refs, exp_refs = refs[:SIDE], refs[SIDE : 2 * SIDE]
    weighted_ref, linear_ref = refs[2 * SIDE :]
    divisor = divisor_ref[...]
    for j in range(WORDS // 128):
        cols = slice(128 * j, 128 * j + 128)
        sums = [read_sum(body_refs, exp_refs, q, cols) for q in range(QUANTITIES)]
        for h in range(2):
            start = 128 * j + WORDS * h
            size = min(128, LAGS - start)
            linear = sums[0][h] / divisor
            real, imag = sums[1][h], sums[2][h]
            weighted = linear * ((real * real + imag * imag) / (divisor * divisor))
            linear_ref[:, start : start + size] = linear[:, :size]
            weighted_ref[:, start : start + size] = weighted[:, :size]


def finish(divisor, messages):
    body = pl.BlockSpec((QUANTITIES * OWNED, WORDS), lambda i: (0, 0))
    exps = pl.BlockSpec((8, 128), lambda i: (QUANTITIES * OWNED // 8, 0))
    out = pl.BlockSpec((OWNED, LAGS), lambda i: (0, 0))
    return pl.pallas_call(
        finish_kernel,
        grid=(1,),
        in_specs=[pl.BlockSpec((OWNED, 128), lambda i: (0, 0))] + [body] * SIDE + [exps] * SIDE,
        out_specs=[out, out],
        out_shape=[jax.ShapeDtypeStruct((OWNED, LAGS), jnp.float32)] * 2,
        compiler_params=params(),
        name="finish",
    )(divisor, *messages, *messages)


def shift(message, step, first):
    moves = []
    for x in range(SIDE):
        for y in range(SIDE):
            for pair in range(8):
                along_x = (pair % 2 == 0) == first
                to_x = (x + step) % SIDE if along_x else x
                to_y = y if along_x else (y + step) % SIDE
                moves.append(((x * SIDE + y) * 8 + pair, (to_x * SIDE + to_y) * 8 + pair))
    return lax.ppermute(message, ("day", "pair"), moves)


def exchange_small(values, axis):
    count = lax.axis_size(axis)
    return lax.all_to_all(jnp.broadcast_to(values[None], (count, *values.shape)), axis, 0, 0, tiled=True)


def stacks(correlations, mask, counts):
    masked = correlations * mask[:, :, None].astype(jnp.bfloat16)
    wide = masked.astype(jnp.float32)
    energy = jnp.sum(jnp.square(wide), axis=(1, 2))
    peak = jnp.max(jnp.abs(wide), axis=(1, 2))
    used_pairs = jnp.sum(mask, axis=1).astype(jnp.float32)
    totals = jnp.sum(exchange_small(jnp.concatenate([energy, used_pairs]), "pair"), axis=0)
    energy, used_pairs = totals[:DAYS], totals[DAYS:]
    weight = lax.rsqrt(energy / (LAGS * jnp.maximum(used_pairs, 1.0)) + 0.1)

    reach = weight * peak
    bounds = jnp.stack(
        [
            jnp.sum(reach),
            jnp.sum(jnp.minimum(1.0, 2.0 * reach)),
            jnp.sum(jnp.minimum(1.0, 2.0 * KERNEL_SUM * reach)),
        ]
    )
    exponent = jnp.ceil(jnp.log2(jnp.maximum(bounds, 1e-30) * 1.001)).astype(jnp.int32)
    scale = TOP * jnp.exp2(-0.5 * exponent.astype(jnp.float32))

    place = lax.axis_index("day")
    x, y = place // SIDE, place % SIDE
    core = lax.axis_index("pair") % 2
    a, b = jnp.arange(SIDE)[:, None], jnp.arange(SIDE)[None, :]
    order = jnp.where(
        core == 0,
        (x + a) % SIDE * SIDE + (y + b) % SIDE,
        (x + b) % SIDE * SIDE + (y + a) % SIDE,
    ).reshape(-1)

    table = kernel_table()

    def chunk(k):
        return terms(k, order, weight, scale, exponent, masked, table)

    def wide_step(k):
        piece = chunk(k)
        return shift(piece, k, True) if k else piece

    def narrow_step(l):
        piece = combine(l, messages)
        return shift(piece, l, False) if l else piece

    far, ahead, behind, own = [wide_step(k) for k in (2, 1, 3, 0)]
    messages = [own, ahead, far, behind]
    far, ahead, behind, own = [narrow_step(l) for l in (2, 1, 3, 0)]
    arrived = [own, ahead, far, behind]
    divisor = jnp.broadcast_to(jnp.maximum(counts.astype(jnp.float32), 1.0)[:, None], (OWNED, 128))
    return tuple(finish(divisor, arrived))


def solution(mesh):
    placed = (P("day", "pair", None), P("day", "pair"), P(("pair", "day")))
    return jax.shard_map(
        stacks,
        mesh=mesh,
        in_specs=placed,
        out_specs=(P(("pair", "day"), None), P(("pair", "day"), None)),
        check_vma=False,
    )
```

time: 234 us -> 138 us (0.59)
  the two profiles are of different devices: /device:TPU:28 before, /device:TPU:0 now
where the time goes in v1:
time: 138 us; the launch traced here: 137 us
  Pallas kernels  49.5 us (36%)
  waiting for transfers between devices  37.7 us (27%)
  local copies, waits for them, and re-layouts  21.1 us (15%)
  starting transfers between devices  15 us (11%)
  other arithmetic  12.8 us (9%)
    pallas_call x4, Pallas kernels, terms(): pl.pallas_call(terms_kernel, grid_spec=pltpu.PrefetchScalarGridSpec(num_s...  42.6 us
    ppermute x6, waiting for transfers between devices, shift(): return lax.ppermute(message, ('day', 'pair'), moves)  37.7 us
    unnamed x7, local copies, waits for them, and re-layouts  20.3 us
    ppermute x6, starting transfers between devices, shift(): return lax.ppermute(message, ('day', 'pair'), moves)  9.53 us
    reduce_max x1, other arithmetic, stacks(): peak = jnp.max(jnp.abs(wide), axis=(1, 2))  8.42 us
    all_to_all x1, starting transfers between devices, exchange_small(): lax.all_to_all(jnp.broadcast_to(values[None], (count, *values.shape)), ax...  5.43 us
    pallas_call x4, Pallas kernels, combine(): pl.pallas_call(combine_kernel, grid=(1,), in_specs=[body] * SIDE + [exps]...  3.92 us
  transfers between devices with their start and end apart: 7, of which 5 were waited for; matrix products, arithmetic and copies ran while one was open for 1% of the time, Pallas kernels for 11%

profile of v1, /device:TPU:0, one launch (start us, length us, event | category | flops | bytes accessed | tf_op | source)
XLA Modules:
  0.0 136.8 jit_solution(15325964214057659555)
XLA Ops:
  0.6 0.9 fusion.19
  1.5 13.7 %copy.7 = bf16[4,512,2001]{2,1,0:T(8,128)(2,1)} copy(bf16[4,512,2001]{1,0,2:T(4,128)(2,1)} %param.3) | data formatting | bytes 16392192 | tf_op args[0]
  15.3 8.4 %fusion.1 = (f32[4]{0:T(128)S(1)}, f32[4]{0:T(128)S(1)}, bf16[4,512,2001]{2,1,0:T(8,128)(2,1)}) fusion(bf16[4,512,2001]{2,1,0:T(8,128)(2,1)} %copy.7, bf16[4,512]{1,0:T(4,128)(2,1)S(1)} %get-tuple-element.12), kind=kLoop, calls=%fused_computation.3 | loop fusion | flops 24588280 | bytes 16396320 | tf_op jit(solution)/shard_map/reduce_max | solution.py:242
  24.4 5.4 %all-to-all-start = ((f32[8,1,8]{2,1,0:T(1,128)}), f32[8,1,8]{2,1,0:T(1,128)S(1)}, u32[]{:S(2)}, u32[]{:S(2)}) async-start(f32[8,1,8]{2,1,0:T(1,128)} %broadcast_in_dim.10), calls=%async_computation | async-start | bytes 8192 | tf_op jit(solution)/shard_map/all_to_all | solution.py:235
  30.6 1.4 %table.1.refs_4_ = bf16[2048,2048]{1,0:T(8,128)(2,1)S(1)} custom-call(f32[8,4096]{1,0:T(8,128)S(1)} %fusion.14.ext_ref), custom_call_target="tpu_custom_call" | custom-call | tf_op jit(solution)/shard_map/table/pallas_call | solution.py:68
  32.1 3.2 %copy-done.1 = bf16[2048,2048]{1,0:T(8,128)(2,1)} copy-done((bf16[2048,2048]{1,0:T(8,128)(2,1)}, bf16[2048,2048]{1,0:T(8,128)(2,1)S(1)}, u32[]{:S(2)}) %copy-start.1) | copy-done | bytes 8388632
  36.0 1.9 %exponential_multiply_fusion = (f32[3]{0:T(128)S(1)}, s32[3]{0:T(128)S(1)}) fusion(f32[1]{0:T(128)} %bitcast.3, f32[1]{0:T(128)} %bitcast.2, f32[1]{0:T(128)} %bitcast.1), kind=kLoop, calls=%fused_computation.37 | loop fusion | flops 30 | bytes 36 | tf_op jit(solution)/shard_map/mul | solution.py:257
  38.0 3.4 %copy-done = bf16[4,512,2001]{2,1,0:T(8,128)(2,1)S(1)} copy-done((bf16[4,512,2001]{2,1,0:T(8,128)(2,1)S(1)}, bf16[4,512,2001]{2,1,0:T(8,128)(2,1)}, u32[]{:S(2)}) %copy-start) | copy-done | bytes 8196120
  41.4 10.6 %terms.7 = s32[392,1024]{1,0:T(8,128)S(1)} custom-call(s32[16]{0:T(128)S(1)} %select_n.91.order_ref, f32[4]{0:T(128)S(1)} %get-tuple-element.9.weight_ref, f32[3]{0:T(128)S(1)} %get-tuple-element.7.scale_ref, s32[3]{0:T(128)S(1)} %get-tuple-element.8.exp_ref, bf16[4,512,2001]{2,1,0:T(8,128)(2,1)S(1)} %copy-done, bf16[4,512,2001]{2,1,0:T(8,128)(2,1)S(1)} %copy-done, ...), custom_call_target="tpu_custom_call" | custom-call | flops 4294967296 | bytes 12582912 | tf_op jit(solution)/shard_map/terms/pallas_call | solution.py:127
  52.0 10.6 %terms.6 = s32[392,1024]{1,0:T(8,128)S(1)} custom-call(s32[16]{0:T(128)S(1)} %select_n.91.order_ref, f32[4]{0:T(128)S(1)} %get-tuple-element.9.weight_ref, f32[3]{0:T(128)S(1)} %get-tuple-element.7.scale_ref, s32[3]{0:T(128)S(1)} %get-tuple-element.8.exp_ref, bf16[4,512,2001]{2,1,0:T(8,128)(2,1)S(1)} %copy-done, bf16[4,512,2001]{2,1,0:T(8,128)(2,1)S(1)} %copy-done, ...), custom_call_target="tpu_custom_call" | custom-call | flops 4294967296 | bytes 12582912 | tf_op jit(solution)/shard_map/terms/pallas_call | solution.py:127
  62.7 10.6 %terms.5 = s32[392,1024]{1,0:T(8,128)S(1)} custom-call(s32[16]{0:T(128)S(1)} %select_n.91.order_ref, f32[4]{0:T(128)S(1)} %get-tuple-element.9.weight_ref, f32[3]{0:T(128)S(1)} %get-tuple-element.7.scale_ref, s32[3]{0:T(128)S(1)} %get-tuple-element.8.exp_ref, bf16[4,512,2001]{2,1,0:T(8,128)(2,1)S(1)} %copy-done, bf16[4,512,2001]{2,1,0:T(8,128)(2,1)S(1)} %copy-done, ...), custom_call_target="tpu_custom_call" | custom-call | flops 4294967296 | bytes 12582912 | tf_op jit(solution)/shard_map/terms/pallas_call | solution.py:127
  73.3 2.8 %collective-permute-start.2 = (s32[392,1024]{1,0:T(8,128)S(1)}, s32[392,1024]{1,0:T(8,128)S(1)}, u32[]{:S(2)}, u32[]{:S(2)}) collective-permute-start(s32[392,1024]{1,0:T(8,128)S(1)} %terms.7), channel_id=1, source_target_pairs={{0,96},{1,25},{2,98},{3,27},{4,100},{5,29},{6,102},{7,31},{8,104},... | collective-permute-start | bytes 4816904 | tf_op jit(solution)/shard_map/ppermute | solution.py:230
  77.8 10.6 %terms.4.refs_0_.refs_4_ = s32[392,1024]{1,0:T(8,128)S(1)} custom-call(s32[16]{0:T(128)S(1)} %select_n.91.order_ref, f32[4]{0:T(128)S(1)} %get-tuple-element.9.weight_ref, f32[3]{0:T(128)S(1)} %get-tuple-element.7.scale_ref, s32[3]{0:T(128)S(1)} %get-tuple-element.8.exp_ref, bf16[4,512,2001]{2,1,0:T(8,128)(2,1)S(1)} %copy-done, ...), custom_call_target="tpu_custom_call" | custom-call | flops 4294967296 | bytes 12582912 | tf_op jit(solution)/shard_map/terms/pallas_call | solution.py:127
  88.5 23.2 %collective-permute-done.2.refs_3_.refs_7_ = s32[392,1024]{1,0:T(8,128)S(1)} collective-permute-done((s32[392,1024]{1,0:T(8,128)S(1)}, s32[392,1024]{1,0:T(8,128)S(1)}, u32[]{:S(2)}, u32[]{:S(2)}) %collective-permute-start.2) | collective-permute-done | bytes 1605664 | tf_op jit(solution)/shard_map/ppermute | solution.py:230
  111.7 3.9 %collective-permute-done.refs_1_.refs_5_ = s32[392,1024]{1,0:T(8,128)S(1)} collective-permute-done((s32[392,1024]{1,0:T(8,128)S(1)}, s32[392,1024]{1,0:T(8,128)S(1)}, u32[]{:S(2)}, u32[]{:S(2)}) %collective-permute-start) | collective-permute-done | bytes 1605664 | tf_op jit(solution)/shard_map/ppermute | solution.py:230
  115.6 1.0 combine.7
  116.6 3.3 %collective-permute-start.5 = (s32[104,1024]{1,0:T(8,128)S(1)}, s32[104,1024]{1,0:T(8,128)S(1)}, u32[]{:S(2)}, u32[]{:S(2)}) collective-permute-start(s32[104,1024]{1,0:T(8,128)S(1)} %combine.7), channel_id=1, source_target_pairs={{0,24},{1,97},{2,26},{3,99},{4,28},{5,101},{6,30},{7,103},{8,0},{9... | collective-permute-start | bytes 1277960 | tf_op jit(solution)/shard_map/ppermute | solution.py:230
  119.9 1.0 combine.6
  121.6 1.0 combine.5
  122.5 1.0 collective-permute-start.3
  123.6 1.0 combine.4.refs_0_.refs_4_
  124.6 5.5 %collective-permute-done.5.refs_3_.refs_7_ = s32[104,1024]{1,0:T(8,128)S(1)} collective-permute-done((s32[104,1024]{1,0:T(8,128)S(1)}, s32[104,1024]{1,0:T(8,128)S(1)}, u32[]{:S(2)}, u32[]{:S(2)}) %collective-permute-start.5) | collective-permute-done | bytes 426016 | tf_op jit(solution)/shard_map/ppermute | solution.py:230
  130.7 4.5 %collective-permute-done.3.refs_1_.refs_5_ = s32[104,1024]{1,0:T(8,128)S(1)} collective-permute-done((s32[104,1024]{1,0:T(8,128)S(1)}, s32[104,1024]{1,0:T(8,128)S(1)}, u32[]{:S(2)}, u32[]{:S(2)}) %collective-permute-start.3) | collective-permute-done | bytes 426016 | tf_op jit(solution)/shard_map/ppermute | solution.py:230
  135.2 1.6 %finish.1 = (f32[32,2001]{1,0:T(8,128)}, f32[32,2001]{1,0:T(8,128)}) custom-call(f32[32,128]{1,0:T(8,128)S(1)} %broadcast_in_dim.9.divisor_ref, s32[104,1024]{1,0:T(8,128)S(1)} %combine.4.refs_0_.refs_4_, s32[104,1024]{1,0:T(8,128)S(1)} %collective-permute-done.3.refs_1_.refs_5_, s32[104,1024]{1,0:T(8,128)S(1)} %collective-permute-done.4.refs_2_.refs_6_, ...), custom_call_target="tpu_custom_call" | custom-call | tf_op jit(solution)/shard_map/finish/pallas_call | solution.py:210
  (21 shorter events, 5.3 us)
Async XLA Ops:
  24.4 11.0 %all-to-all-start = ((f32[8,1,8]{2,1,0:T(1,128)}), f32[8,1,8]{2,1,0:T(1,128)S(1)}, u32[]{:S(2)}, u32[]{:S(2)}) async-start(f32[8,1,8]{2,1,0:T(1,128)} %broadcast_in_dim.10), calls=%async_computation | async-start | bytes 8192 | tf_op jit(solution)/shard_map/all_to_all | solution.py:235
  32.1 3.2 %copy-start.1 = (bf16[2048,2048]{1,0:T(8,128)(2,1)}, bf16[2048,2048]{1,0:T(8,128)(2,1)S(1)}, u32[]{:S(2)}) copy-start(bf16[2048,2048]{1,0:T(8,128)(2,1)S(1)} %table.1.refs_4_) | copy-start | bytes 25165828
  38.0 3.4 %copy-start = (bf16[4,512,2001]{2,1,0:T(8,128)(2,1)S(1)}, bf16[4,512,2001]{2,1,0:T(8,128)(2,1)}, u32[]{:S(2)}) copy-start(bf16[4,512,2001]{2,1,0:T(8,128)(2,1)} %get-tuple-element.10.refs_0_.refs_1_.refs_2_.refs_3_) | copy-start | bytes 24588292
  73.3 38.4 %collective-permute-start.2 = (s32[392,1024]{1,0:T(8,128)S(1)}, s32[392,1024]{1,0:T(8,128)S(1)}, u32[]{:S(2)}, u32[]{:S(2)}) collective-permute-start(s32[392,1024]{1,0:T(8,128)S(1)} %terms.7), channel_id=1, source_target_pairs={{0,96},{1,25},{2,98},{3,27},{4,100},{5,29},{6,102},{7,31},{8,104},... | collective-permute-start | bytes 4816904 | tf_op jit(solution)/shard_map/ppermute | solution.py:230
  76.1 35.5 %collective-permute-start.1 = (s32[392,1024]{1,0:T(8,128)S(1)}, s32[392,1024]{1,0:T(8,128)S(1)}, u32[]{:S(2)}, u32[]{:S(2)}) collective-permute-start(s32[392,1024]{1,0:T(8,128)S(1)} %terms.6), channel_id=1, source_target_pairs={{0,64},{1,17},{2,66},{3,19},{4,68},{5,21},{6,70},{7,23},{8,72},{9,... | collective-permute-start | bytes 4816904 | tf_op jit(solution)/shard_map/ppermute | solution.py:230
  76.9 38.7 %collective-permute-start = (s32[392,1024]{1,0:T(8,128)S(1)}, s32[392,1024]{1,0:T(8,128)S(1)}, u32[]{:S(2)}, u32[]{:S(2)}) collective-permute-start(s32[392,1024]{1,0:T(8,128)S(1)} %terms.5), channel_id=1, source_target_pairs={{0,32},{1,9},{2,34},{3,11},{4,36},{5,13},{6,38},{7,15},{8,40},{9,1... | collective-permute-start | bytes 4816904 | tf_op jit(solution)/shard_map/ppermute | solution.py:230
  116.6 13.5 %collective-permute-start.5 = (s32[104,1024]{1,0:T(8,128)S(1)}, s32[104,1024]{1,0:T(8,128)S(1)}, u32[]{:S(2)}, u32[]{:S(2)}) collective-permute-start(s32[104,1024]{1,0:T(8,128)S(1)} %combine.7), channel_id=1, source_target_pairs={{0,24},{1,97},{2,26},{3,99},{4,28},{5,101},{6,30},{7,103},{8,0},{9... | collective-permute-start | bytes 1277960 | tf_op jit(solution)/shard_map/ppermute | solution.py:230
  120.8 2.7 %copy-start.2 = (s32[32]{0:T(128)S(1)}, s32[32]{0:T(128)}, u32[]{:S(2)}) copy-start(s32[32]{0:T(128)} %param.5) | copy-start | bytes 388
  120.9 9.8 %collective-permute-start.4 = (s32[104,1024]{1,0:T(8,128)S(1)}, s32[104,1024]{1,0:T(8,128)S(1)}, u32[]{:S(2)}, u32[]{:S(2)}) collective-permute-start(s32[104,1024]{1,0:T(8,128)S(1)} %combine.6), channel_id=1, source_target_pairs={{0,16},{1,65},{2,18},{3,67},{4,20},{5,69},{6,22},{7,71},{8,24},{9,... | collective-permute-start | bytes 1277960 | tf_op jit(solution)/shard_map/ppermute | solution.py:230
  122.5 12.6 %collective-permute-start.3 = (s32[104,1024]{1,0:T(8,128)S(1)}, s32[104,1024]{1,0:T(8,128)S(1)}, u32[]{:S(2)}, u32[]{:S(2)}) collective-permute-start(s32[104,1024]{1,0:T(8,128)S(1)} %combine.5), channel_id=1, source_target_pairs={{0,8},{1,33},{2,10},{3,35},{4,12},{5,37},{6,14},{7,39},{8,16},{9,4... | collective-permute-start | bytes 1277960 | tf_op jit(solution)/shard_map/ppermute | solution.py:230

commit v2 on v1

v2 whole, which is shorter than its diff:
```python
import functools

import jax
import jax.numpy as jnp
from jax import lax
from jax.experimental import pallas as pl
from jax.experimental.pallas import tpu as pltpu
from jax.sharding import PartitionSpec as P


LAGS = 2001
WIDTH = 2048
WORDS = WIDTH // 2
OWNED = 32
DAYS = 4
SIDE = 4
QUANTITIES = 3
TOP = 32766.0
KERNEL_SUM = 6.0
MB = 1 << 20


def params(**settings):
    return pltpu.CompilerParams(**{"vmem_limit_bytes": 32 * MB, **settings})


def encode(value, scale):
    root = value * lax.rsqrt(jnp.abs(value) + 1e-36)
    return (root * scale + 32768.5).astype(jnp.int32)


def pack(low, high):
    return low | (high << 16)


def unpack(word):
    low = (word & 0xFFFF).astype(jnp.float32) - 32768.0
    high = (lax.shift_right_logical(word, 16)).astype(jnp.float32) - 32768.0
    return low * jnp.abs(low), high * jnp.abs(high)


def unit(exponent):
    return jnp.exp2(exponent.astype(jnp.float32)) * (1.0 / (TOP * TOP))


def first_shifts():
    row = lax.broadcasted_iota(jnp.int32, (8, 2 * WIDTH), 0)
    col = lax.broadcasted_iota(jnp.int32, (8, 2 * WIDTH), 1)
    offset = (col - row - WIDTH + 2 * LAGS) % LAGS
    offset = jnp.where(offset > LAGS // 2, offset - LAGS, offset)
    angle = jnp.pi * offset.astype(jnp.float32) / LAGS
    parity = 1.0 - 2.0 * (offset % 2).astype(jnp.float32)
    sine = jnp.where(offset == 0, 1.0, jnp.sin(angle))
    values = jnp.where(offset == 0, 0.0, (jnp.cos(angle) - parity) / (LAGS * sine))
    return values.astype(jnp.bfloat16).astype(jnp.float32)


def fill_table(shifts_ref, table_ref, rolled_ref):
    for q in range(16):
        first = pltpu.roll(shifts_ref[...], 16 * q, 1)
        second = pltpu.roll(shifts_ref[...], 16 * q + 8, 1)
        rolled_ref[16 * q : 16 * q + 16, :] = jnp.concatenate([first, second], 0).astype(jnp.bfloat16)
    for q in range(8):
        for n in range(8):
            for h in range(2):
                start = 128 * (n + 8 * h) - 256 * q + WIDTH
                table_ref[n, 256 * q : 256 * q + 256, 128 * h : 128 * h + 128] = rolled_ref[:, start : start + 128]


TILES = WIDTH // 128
GROUPS = 16


def position(owner, place):
    x, y, core = place >> 3, (place >> 1) & 3, place & 1
    along_x, along_y = (owner // SIDE - x) & 3, (owner % SIDE - y) & 3
    return jnp.where(core == 0, along_x * SIDE + along_y, along_y * SIDE + along_x)


def rows_kernel(
    place_ref, input_ref, mask_ref, shifts_ref, out_ref, table_ref, stats_ref, peak_ref, *scratch
):
    held_ref, square_ref, most_ref, rolled_ref, sems = scratch
    place = place_ref[0]
    last = (LAGS - 128 * (TILES - 1)) * GROUPS

    def fetch(j, size):
        return pltpu.make_async_copy(
            input_ref.at[pl.ds(j * 128 * GROUPS, size), :], held_ref.at[j, pl.ds(0, size), :], sems.at[j]
        )

    for j in range(TILES):
        fetch(j, 128 * GROUPS if j < TILES - 1 else last).start()
    fill_table(shifts_ref, table_ref, rolled_ref)
    held_ref[TILES - 1, last:, :] = jnp.zeros((128 * GROUPS - last, 128), jnp.bfloat16)
    square_ref[...] = jnp.zeros_like(square_ref)
    most_ref[...] = jnp.zeros_like(most_ref)
    row = lax.broadcasted_iota(jnp.int32, (256, 256), 0)
    col = lax.broadcasted_iota(jnp.int32, (256, 256), 1)
    select = ((row // 16 == col % 16) & (row % 16 == col // 16)).astype(jnp.float32).astype(jnp.bfloat16)
    places = [position(owner, place) for owner in range(SIDE * SIDE)]

    def tile(j):
        parts = []
        for b in range(4):
            first = held_ref[j, 512 * b : 512 * b + 256, :]
            second = held_ref[j, 512 * b + 256 : 512 * b + 512, :]
            parts.append(
                jnp.dot(select, jnp.concatenate([first, second], 1), preferred_element_type=jnp.float32)
            )
        for t in range(4):
            for d in range(DAYS):
                at = 16 * (t * DAYS + d)
                pieces = [p[at : at + 16, 128 * h : 128 * h + 128] for p in parts for h in range(2)]
                used = mask_ref[d : d + 1, 128 * t : 128 * t + 128].astype(jnp.float32)
                values = jnp.concatenate(pieces, 0) * used
                squares = (values * values).reshape(16, 8, 128)
                square_ref[d] += jnp.sum(squares, axis=0)
                most_ref[d] = jnp.maximum(most_ref[d], jnp.max(squares, axis=0))
                turned = values.T.astype(jnp.bfloat16)
                for i in range(4):
                    lanes = pl.ds(pl.multiple_of(j * 128, 128), 128)
                    out_ref[places[t * 4 + i], d, :, lanes] = turned[OWNED * i : OWNED * i + OWNED, :]

    def step(j, carry):
        fetch(j, 128 * GROUPS).wait()
        tile(j)
        return carry

    lax.fori_loop(0, TILES - 1, step, 0)
    fetch(TILES - 1, last).wait()
    tile(TILES - 1)

    row = lax.broadcasted_iota(jnp.int32, (8, 128), 0)
    stats = peaks = jnp.zeros((8, 128), jnp.float32)
    for d in range(DAYS):
        stats = jnp.where(row == d, jnp.sum(square_ref[d]), stats)
        stats = jnp.where(row == DAYS + d, jnp.sum(mask_ref[d : d + 1, :].astype(jnp.float32)), stats)
        peaks = jnp.where(row == d, jnp.max(most_ref[d]), peaks)
    peak_ref[...] = peaks
    for i in range(8):
        stats_ref[i] = stats


def ordered_rows(place, correlations, mask):
    stored = correlations.reshape(DAYS, 4, 128, LAGS).transpose(3, 1, 0, 2).reshape(LAGS * GROUPS, 128)
    vmem = pl.BlockSpec(memory_space=pltpu.VMEM)
    return pl.pallas_call(
        rows_kernel,
        in_specs=[
            pl.BlockSpec(memory_space=pltpu.SMEM),
            pl.BlockSpec(memory_space=pltpu.HBM),
            vmem,
            vmem,
        ],
        out_specs=[vmem] * 4,
        out_shape=[
            jax.ShapeDtypeStruct((SIDE * SIDE, DAYS, OWNED, WIDTH), jnp.bfloat16),
            jax.ShapeDtypeStruct((8, WIDTH, 256), jnp.bfloat16),
            jax.ShapeDtypeStruct((8, 8, 128), jnp.float32),
            jax.ShapeDtypeStruct((8, 128), jnp.float32),
        ],
        scratch_shapes=[
            pltpu.VMEM((TILES, 128 * GROUPS, 128), jnp.bfloat16),
            pltpu.VMEM((DAYS, 8, 128), jnp.float32),
            pltpu.VMEM((DAYS, 8, 128), jnp.float32),
            pltpu.VMEM((256, 2 * WIDTH), jnp.bfloat16),
            pltpu.SemaphoreType.DMA((TILES,)),
        ],
        compiler_params=params(vmem_limit_bytes=28 * MB),
        name="rows",
    )(place, pltpu.with_memory_space_constraint(stored, pltpu.HBM), mask, first_shifts())


def terms_kernel(k, rows_ref, table_ref, stats_ref, peak_ref, out_ref, even_ref, odd_ref):
    total = jnp.sum(stats_ref[...], axis=0)
    energy, used = total[:DAYS, :], total[DAYS:, :]
    weight = lax.rsqrt(energy / (LAGS * jnp.maximum(used, 1.0)) + 0.1)
    reach = weight * jnp.sqrt(peak_ref[:DAYS, :])
    bounds = [
        jnp.sum(reach, axis=0, keepdims=True),
        jnp.sum(jnp.minimum(1.0, 2.0 * reach), axis=0, keepdims=True),
        jnp.sum(jnp.minimum(1.0, 2.0 * KERNEL_SUM * reach), axis=0, keepdims=True),
    ]
    powers = [jnp.ceil(jnp.log(jnp.maximum(v, 1e-30) * 1.001) * 1.4426951) for v in bounds]
    scale = [TOP * jnp.exp2(-0.5 * p) for p in powers]
    row = lax.broadcasted_iota(jnp.int32, (8, 128), 0)
    exponents = jnp.where(row == 0, powers[0], jnp.where(row == 1, powers[1], powers[2])).astype(jnp.int32)
    for n in range(WORDS // 128):
        out_ref[SIDE * QUANTITIES * OWNED :, 128 * n : 128 * n + 128] = exponents
    weights = [weight[d : d + 1, :] for d in range(DAYS)]

    def product(n, to_ref):
        to_ref[...] = jnp.dot(rows_ref[k], table_ref[n], preferred_element_type=jnp.float32)

    def finish_block(n, hilbert_ref):
        for l in range(SIDE):
            codes = []
            for h in range(2):
                lanes = pl.ds(pl.multiple_of(n * 128 + h * WORDS, 128), 128)
                linear = real = imag = None
                for d in range(DAYS):
                    at = (l * DAYS + d) * OWNED
                    real_part = rows_ref[k, at : at + OWNED, lanes].astype(jnp.float32) * weights[d]
                    imag_part = hilbert_ref[at : at + OWNED, 128 * h : 128 * h + 128] * weights[d]
                    inverse = lax.rsqrt(real_part * real_part + imag_part * imag_part + 0.25)
                    a, b = real_part * inverse, imag_part * inverse
                    linear = real_part if d == 0 else linear + real_part
                    real = a if d == 0 else real + a
                    imag = b if d == 0 else imag + b
                codes.append([encode(v, scale[q]) for q, v in enumerate((linear, real, imag))])
            for q in range(QUANTITIES):
                at = (l * QUANTITIES + q) * OWNED
                out_ref[at : at + OWNED, pl.ds(pl.multiple_of(n * 128, 128), 128)] = pack(codes[0][q], codes[1][q])

    def step(i, carry):
        product(2 * i + 1, odd_ref)
        finish_block(2 * i, even_ref)
        product(2 * i + 2, even_ref)
        finish_block(2 * i + 1, odd_ref)
        return carry

    product(0, even_ref)
    lax.fori_loop(0, 3, step, 0)
    product(7, odd_ref)
    finish_block(6, even_ref)
    finish_block(7, odd_ref)


def terms(k, rows, table, stats, peak):
    count = SIDE * QUANTITIES * OWNED + 8
    vmem = pl.BlockSpec(memory_space=pltpu.VMEM)
    return pl.pallas_call(
        functools.partial(terms_kernel, k),
        in_specs=[vmem] * 4,
        out_specs=vmem,
        out_shape=jax.ShapeDtypeStruct((count, WORDS), jnp.int32),
        scratch_shapes=[pltpu.VMEM((SIDE * DAYS * OWNED, 256), jnp.float32)] * 2,
        compiler_params=params(vmem_limit_bytes=24 * MB),
        cost_estimate=pl.CostEstimate(
            flops=2 * SIDE * DAYS * OWNED * WIDTH * WIDTH, bytes_accessed=12 * MB, transcendentals=0
        ),
        name="terms",
    )(rows, table, stats, peak)


def read_sum(body_refs, exp_refs, q, cols):
    low = high = None
    for body, exp in zip(body_refs, exp_refs):
        k = unit(exp[q : q + 1, :])
        a, b = unpack(body[q * OWNED : (q + 1) * OWNED, cols])
        low = a * k if low is None else low + a * k
        high = b * k if high is None else high + b * k
    return low, high


def combine_kernel(*refs):
    body_refs, exp_refs, out_ref = refs[:SIDE], refs[SIDE : 2 * SIDE], refs[2 * SIDE]
    top = exp_refs[0][...]
    for exp in exp_refs[1:]:
        top = jnp.maximum(top, exp[...])
    top = top + 2
    scale = jnp.exp2(-0.5 * top.astype(jnp.float32)) * TOP
    for j in range(WORDS // 128):
        cols = slice(128 * j, 128 * j + 128)
        for q in range(QUANTITIES):
            low, high = read_sum(body_refs, exp_refs, q, cols)
            s = scale[q : q + 1, :]
            out_ref[q * OWNED : (q + 1) * OWNED, cols] = pack(encode(low, s), encode(high, s))
        out_ref[QUANTITIES * OWNED :, cols] = top


def combine(l, messages):
    body = pl.BlockSpec((QUANTITIES * OWNED, WORDS), lambda i: (l, 0))
    exps = pl.BlockSpec((8, 128), lambda i: (SIDE * QUANTITIES * OWNED // 8, 0))
    rows = QUANTITIES * OWNED + 8
    return pl.pallas_call(
        combine_kernel,
        grid=(1,),
        in_specs=[body] * SIDE + [exps] * SIDE,
        out_specs=pl.BlockSpec((rows, WORDS), lambda i: (0, 0)),
        out_shape=jax.ShapeDtypeStruct((rows, WORDS), jnp.int32),
        compiler_params=params(),
        cost_estimate=pl.CostEstimate(flops=2 * MB, bytes_accessed=2 * MB, transcendentals=0),
        name="combine",
    )(*messages, *messages)


def finish_kernel(divisor_ref, *refs):
    body_refs, exp_refs = refs[:SIDE], refs[SIDE : 2 * SIDE]
    weighted_ref, linear_ref = refs[2 * SIDE :]
    divisor = divisor_ref[...]
    for j in range(WORDS // 128):
        cols = slice(128 * j, 128 * j + 128)
        sums = [read_sum(body_refs, exp_refs, q, cols) for q in range(QUANTITIES)]
        for h in range(2):
            start = 128 * j + WORDS * h
            size = min(128, LAGS - start)
            linear = sums[0][h] / divisor
            real, imag = sums[1][h], sums[2][h]
            weighted = linear * ((real * real + imag * imag) / (divisor * divisor))
            linear_ref[:, start : start + size] = linear[:, :size]
            weighted_ref[:, start : start + size] = weighted[:, :size]


def finish(divisor, messages):
    body = pl.BlockSpec((QUANTITIES * OWNED, WORDS), lambda i: (0, 0))
    exps = pl.BlockSpec((8, 128), lambda i: (QUANTITIES * OWNED // 8, 0))
    out = pl.BlockSpec((OWNED, LAGS), lambda i: (0, 0))
    return pl.pallas_call(
        finish_kernel,
        grid=(1,),
        in_specs=[pl.BlockSpec((OWNED, 128), lambda i: (0, 0))] + [body] * SIDE + [exps] * SIDE,
        out_specs=[out, out],
        out_shape=[jax.ShapeDtypeStruct((OWNED, LAGS), jnp.float32)] * 2,
        compiler_params=params(),
        name="finish",
    )(divisor, *messages, *messages)


def shift(message, step, first):
    moves = []
    for x in range(SIDE):
        for y in range(SIDE):
            for pair in range(8):
                along_x = (pair % 2 == 0) == first
                to_x = (x + step) % SIDE if along_x else x
                to_y = y if along_x else (y + step) % SIDE
                moves.append(((x * SIDE + y) * 8 + pair, (to_x * SIDE + to_y) * 8 + pair))
    return lax.ppermute(message, ("day", "pair"), moves)


def stacks(correlations, mask, counts):
    place = (lax.axis_index("day") * 2 + lax.axis_index("pair") % 2).reshape(1)
    rows, table, stats, peak = ordered_rows(place, correlations, mask)
    rows = rows.reshape(SIDE, SIDE * DAYS * OWNED, WIDTH)
    stats = lax.all_to_all(stats, "pair", 0, 0, tiled=True)

    def wide_step(k):
        piece = terms(k, rows, table, stats, peak)
        return shift(piece, k, True) if k else piece

    def narrow_step(l):
        piece = combine(l, messages)
        return shift(piece, l, False) if l else piece

    far, ahead, behind, own = [wide_step(k) for k in (2, 1, 3, 0)]
    messages = [own, ahead, far, behind]
    far, ahead, behind, own = [narrow_step(l) for l in (2, 1, 3, 0)]
    arrived = [own, ahead, far, behind]
    divisor = jnp.broadcast_to(jnp.maximum(counts.astype(jnp.float32), 1.0)[:, None], (OWNED, 128))
    return tuple(finish(divisor, arrived))


def solution(mesh):
    placed = (P("day", "pair", None), P("day", "pair"), P(("pair", "day")))
    return jax.shard_map(
        stacks,
        mesh=mesh,
        in_specs=placed,
        out_specs=(P(("pair", "day"), None), P(("pair", "day"), None)),
        check_vma=False,
    )
```

time: 138 us -> 102 us (0.74)
  local copies, waits for them, and re-layouts: 21.1 us -> 0.77 us
  other arithmetic: 12.8 us -> 0.65 us
  blocking collectives: 0 us -> 10.7 us
  starting transfers between devices: 15 us -> 9.65 us
  waiting for transfers between devices: 37.7 us -> 33.7 us
  Pallas kernels: 49.5 us -> 45.7 us
    unnamed x7 -> x4, local copies, waits for them, and re-layouts: 20.3 us -> 0.7 us
    all_to_all x0 -> x1, blocking collectives: none -> 10.7 us  [stacks(): stats = lax.all_to_all(stats, 'pair', 0, 0, tiled=True)]
    reduce_max x1 -> x0, other arithmetic: 8.42 us -> none  [stacks(): peak = jnp.max(jnp.abs(wide), axis=(1, 2))]
    all_to_all x1 -> x0, starting transfers between devices: 5.43 us -> none  [exchange_small(): lax.all_to_all(jnp.broadcast_to(values[None], (count, *values.shape)), ax...]
    ppermute x6, waiting for transfers between devices: 37.7 us -> 33.7 us  [shift(): return lax.ppermute(message, ('day', 'pair'), moves)]
    pallas_call x5, Pallas kernels: 44 us -> 40.2 us  [the longest x4 29 us: terms(): pl.pallas_call(functools.partial(terms_kernel, k), in_specs=[vmem] * 4, o...]
    mul x1 -> x0, other arithmetic: 1.94 us -> none  [stacks(): scale = TOP * jnp.exp2(-0.5 * exponent.astype(jnp.float32))]
    reduce_sum x3 -> x0, other arithmetic: 1.6 us -> none  [the longest x1 0.89 us: stacks(): used_pairs = jnp.sum(mask, axis=1).astype(jnp.float32)]
  transfers between devices with their start and end apart: 7 -> 6, of which waited for: 5 -> 5; matrix products, arithmetic and copies ran while one was open for 1% -> 0% of each run, Pallas kernels for 11% -> 24%
where the time goes in v2:
time: 102 us
  Pallas kernels  45.7 us (45%)
  waiting for transfers between devices  33.7 us (33%)
  blocking collectives  10.7 us (10%)
  starting transfers between devices  9.65 us (9%)
    ppermute x6, waiting for transfers between devices, shift(): return lax.ppermute(message, ('day', 'pair'), moves)  33.7 us
    pallas_call x4, Pallas kernels, terms(): pl.pallas_call(functools.partial(terms_kernel, k), in_specs=[vmem] * 4, o...  29 us
    pallas_call x1, Pallas kernels, ordered_rows(): pl.pallas_call(rows_kernel, in_specs=[pl.BlockSpec(memory_space=pltpu.SME...  11.1 us
    all_to_all x1, blocking collectives, stacks(): stats = lax.all_to_all(stats, 'pair', 0, 0, tiled=True)  10.7 us
    ppermute x6, starting transfers between devices, shift(): return lax.ppermute(message, ('day', 'pair'), moves)  9.65 us
    pallas_call x4, Pallas kernels, combine(): pl.pallas_call(combine_kernel, grid=(1,), in_specs=[body] * SIDE + [exps]...  3.92 us
  transfers between devices with their start and end apart: 6, of which 5 were waited for; matrix products, arithmetic and copies ran while one was open for 0% of the time, Pallas kernels for 24%

profile of v2, /device:TPU:0, one launch (start us, length us, event | category | flops | bytes accessed | tf_op | source)
XLA Modules:
  0.0 101.9 jit_solution(16894192461869972171)
XLA Ops:
  0.6 0.6 fusion.12.shifts_ref
  1.3 0.7 copy-done
  2.0 11.1 %rows.1 = (bf16[16,4,32,2048]{3,2,1,0:T(8,128)(2,1)S(1)}, bf16[8,2048,256]{2,1,0:T(8,128)(2,1)S(1)}, f32[8,8,128]{2,1,0:T(8,128)S(1)}, f32[8,128]{1,0:T(8,128)S(1)}) custom-call(s32[1]{0:T(128)} %bitcast.place_ref, bf16[32016,128]{1,0:T(8,128)(2,1)} %bitcast.11, s32[4,512]{1,0:T(4,128)S(1)} %copy-done, f32[8,4096]{1,0:T(8,128)S(1)} %fusion.12.shifts_ref), custom_call_target="tpu_custom_call" | custom-call | tf_op jit(solution)/shard_map/rows/pallas_call | solution.py:148
  13.2 10.7 %all_to_all.5.stats_ref = f32[8,8,128]{2,1,0:T(8,128)S(1)} all-to-all(f32[8,8,128]{2,1,0:T(8,128)S(1)} %get-tuple-element.8), channel_id=1, replica_groups=mesh['day'=16,'pair'=8] {'pair'}, dimensions={0} | all-to-all | bytes 65536 | tf_op jit(solution)/shard_map/all_to_all | solution.py:337
  23.8 7.3 %terms.7 = s32[392,1024]{1,0:T(8,128)S(1)} custom-call(bf16[4,512,2048]{2,1,0:T(8,128)(2,1)S(1)} %bitcast.7, bf16[8,2048,256]{2,1,0:T(8,128)(2,1)S(1)} %get-tuple-element.7.table_ref, f32[8,8,128]{2,1,0:T(8,128)S(1)} %all_to_all.5.stats_ref, f32[8,128]{1,0:T(8,128)S(1)} %get-tuple-element.9.peak_ref), custom_call_target="tpu_custom_call" | custom-call | flops 4294967296 | bytes 12582912 | tf_op jit(solution)/shard_map/terms/pallas_call | solution.py:233
  31.1 2.8 %collective-permute-start.2 = (s32[392,1024]{1,0:T(8,128)S(1)}, s32[392,1024]{1,0:T(8,128)S(1)}, u32[]{:S(2)}, u32[]{:S(2)}) collective-permute-start(s32[392,1024]{1,0:T(8,128)S(1)} %terms.7), channel_id=1, source_target_pairs={{0,96},{1,25},{2,98},{3,27},{4,100},{5,29},{6,102},{7,31},{8,104},... | collective-permute-start | bytes 4816904 | tf_op jit(solution)/shard_map/ppermute | solution.py:330
  33.9 7.3 %terms.6 = s32[392,1024]{1,0:T(8,128)S(1)} custom-call(bf16[4,512,2048]{2,1,0:T(8,128)(2,1)S(1)} %bitcast.8, bf16[8,2048,256]{2,1,0:T(8,128)(2,1)S(1)} %get-tuple-element.7.table_ref, f32[8,8,128]{2,1,0:T(8,128)S(1)} %all_to_all.5.stats_ref, f32[8,128]{1,0:T(8,128)S(1)} %get-tuple-element.9.peak_ref), custom_call_target="tpu_custom_call" | custom-call | flops 4294967296 | bytes 12582912 | tf_op jit(solution)/shard_map/terms/pallas_call | solution.py:233
  41.2 1.1 %collective-permute-start.1 = (s32[392,1024]{1,0:T(8,128)S(1)}, s32[392,1024]{1,0:T(8,128)S(1)}, u32[]{:S(2)}, u32[]{:S(2)}) collective-permute-start(s32[392,1024]{1,0:T(8,128)S(1)} %terms.6), channel_id=1, source_target_pairs={{0,64},{1,17},{2,66},{3,19},{4,68},{5,21},{6,70},{7,23},{8,72},{9,... | collective-permute-start | bytes 4816904 | tf_op jit(solution)/shard_map/ppermute | solution.py:330
  42.2 7.3 %terms.5 = s32[392,1024]{1,0:T(8,128)S(1)} custom-call(bf16[4,512,2048]{2,1,0:T(8,128)(2,1)S(1)} %bitcast.9, bf16[8,2048,256]{2,1,0:T(8,128)(2,1)S(1)} %get-tuple-element.7.table_ref, f32[8,8,128]{2,1,0:T(8,128)S(1)} %all_to_all.5.stats_ref, f32[8,128]{1,0:T(8,128)S(1)} %get-tuple-element.9.peak_ref), custom_call_target="tpu_custom_call" | custom-call | flops 4294967296 | bytes 12582912 | tf_op jit(solution)/shard_map/terms/pallas_call | solution.py:233
  49.5 1.0 collective-permute-start
  50.5 7.3 %terms.4.refs_0_.refs_4_ = s32[392,1024]{1,0:T(8,128)S(1)} custom-call(bf16[4,512,2048]{2,1,0:T(8,128)(2,1)S(1)} %bitcast.10, bf16[8,2048,256]{2,1,0:T(8,128)(2,1)S(1)} %get-tuple-element.7.table_ref, f32[8,8,128]{2,1,0:T(8,128)S(1)} %all_to_all.5.stats_ref, f32[8,128]{1,0:T(8,128)S(1)} %get-tuple-element.9.peak_ref), custom_call_target="tpu_custom_call" | custom-call | flops 4294967296 | bytes 12582912 | tf_op jit(solution)/shard_map/terms/pallas_call | solution.py:233
  57.7 11.7 %collective-permute-done.2.refs_3_.refs_7_ = s32[392,1024]{1,0:T(8,128)S(1)} collective-permute-done((s32[392,1024]{1,0:T(8,128)S(1)}, s32[392,1024]{1,0:T(8,128)S(1)}, u32[]{:S(2)}, u32[]{:S(2)}) %collective-permute-start.2) | collective-permute-done | bytes 1605664 | tf_op jit(solution)/shard_map/ppermute | solution.py:330
  69.4 11.5 %collective-permute-done.refs_1_.refs_5_ = s32[392,1024]{1,0:T(8,128)S(1)} collective-permute-done((s32[392,1024]{1,0:T(8,128)S(1)}, s32[392,1024]{1,0:T(8,128)S(1)}, u32[]{:S(2)}, u32[]{:S(2)}) %collective-permute-start) | collective-permute-done | bytes 1605664 | tf_op jit(solution)/shard_map/ppermute | solution.py:330
  80.9 1.0 combine.7
  81.9 3.1 %collective-permute-start.5 = (s32[104,1024]{1,0:T(8,128)S(1)}, s32[104,1024]{1,0:T(8,128)S(1)}, u32[]{:S(2)}, u32[]{:S(2)}) collective-permute-start(s32[104,1024]{1,0:T(8,128)S(1)} %combine.7), channel_id=1, source_target_pairs={{0,24},{1,97},{2,26},{3,99},{4,28},{5,101},{6,30},{7,103},{8,0},{9... | collective-permute-start | bytes 1277960 | tf_op jit(solution)/shard_map/ppermute | solution.py:330
  85.0 1.0 combine.6
  86.0 0.7 collective-permute-start.4
  86.7 1.0 combine.5
  87.7 1.0 %collective-permute-start.3 = (s32[104,1024]{1,0:T(8,128)S(1)}, s32[104,1024]{1,0:T(8,128)S(1)}, u32[]{:S(2)}, u32[]{:S(2)}) collective-permute-start(s32[104,1024]{1,0:T(8,128)S(1)} %combine.5), channel_id=1, source_target_pairs={{0,8},{1,33},{2,10},{3,35},{4,12},{5,37},{6,14},{7,39},{8,16},{9,4... | collective-permute-start | bytes 1277960 | tf_op jit(solution)/shard_map/ppermute | solution.py:330
  88.7 1.0 combine.4.refs_0_.refs_4_
  89.7 5.5 %collective-permute-done.5.refs_3_.refs_7_ = s32[104,1024]{1,0:T(8,128)S(1)} collective-permute-done((s32[104,1024]{1,0:T(8,128)S(1)}, s32[104,1024]{1,0:T(8,128)S(1)}, u32[]{:S(2)}, u32[]{:S(2)}) %collective-permute-start.5) | collective-permute-done | bytes 426016 | tf_op jit(solution)/shard_map/ppermute | solution.py:330
  95.2 0.6 collective-permute-done.4.refs_2_.refs_6_
  95.8 4.5 %collective-permute-done.3.refs_1_.refs_5_ = s32[104,1024]{1,0:T(8,128)S(1)} collective-permute-done((s32[104,1024]{1,0:T(8,128)S(1)}, s32[104,1024]{1,0:T(8,128)S(1)}, u32[]{:S(2)}, u32[]{:S(2)}) %collective-permute-start.3) | collective-permute-done | bytes 426016 | tf_op jit(solution)/shard_map/ppermute | solution.py:330
  100.3 1.6 %finish.1 = (f32[32,2001]{1,0:T(8,128)}, f32[32,2001]{1,0:T(8,128)}) custom-call(f32[32,128]{1,0:T(8,128)S(1)} %broadcast_in_dim.11.divisor_ref, s32[104,1024]{1,0:T(8,128)S(1)} %combine.4.refs_0_.refs_4_, s32[104,1024]{1,0:T(8,128)S(1)} %collective-permute-done.3.refs_1_.refs_5_, s32[104,1024]{1,0:T(8,128)S(1)} %collective-permute-done.4.refs_2_.refs_6_, ...), custom_call_target="tpu_custom_call" | custom-call | tf_op jit(solution)/shard_map/finish/pallas_call | solution.py:310
  (6 shorter events, 0.1 us)
Async XLA Ops:
  1.3 0.7 copy-start
  31.1 38.3 %collective-permute-start.2 = (s32[392,1024]{1,0:T(8,128)S(1)}, s32[392,1024]{1,0:T(8,128)S(1)}, u32[]{:S(2)}, u32[]{:S(2)}) collective-permute-start(s32[392,1024]{1,0:T(8,128)S(1)} %terms.7), channel_id=1, source_target_pairs={{0,96},{1,25},{2,98},{3,27},{4,100},{5,29},{6,102},{7,31},{8,104},... | collective-permute-start | bytes 4816904 | tf_op jit(solution)/shard_map/ppermute | solution.py:330
  41.2 28.3 %collective-permute-start.1 = (s32[392,1024]{1,0:T(8,128)S(1)}, s32[392,1024]{1,0:T(8,128)S(1)}, u32[]{:S(2)}, u32[]{:S(2)}) collective-permute-start(s32[392,1024]{1,0:T(8,128)S(1)} %terms.6), channel_id=1, source_target_pairs={{0,64},{1,17},{2,66},{3,19},{4,68},{5,21},{6,70},{7,23},{8,72},{9,... | collective-permute-start | bytes 4816904 | tf_op jit(solution)/shard_map/ppermute | solution.py:330
  49.5 31.4 %collective-permute-start = (s32[392,1024]{1,0:T(8,128)S(1)}, s32[392,1024]{1,0:T(8,128)S(1)}, u32[]{:S(2)}, u32[]{:S(2)}) collective-permute-start(s32[392,1024]{1,0:T(8,128)S(1)} %terms.5), channel_id=1, source_target_pairs={{0,32},{1,9},{2,34},{3,11},{4,36},{5,13},{6,38},{7,15},{8,40},{9,1... | collective-permute-start | bytes 4816904 | tf_op jit(solution)/shard_map/ppermute | solution.py:330
  81.9 13.3 %collective-permute-start.5 = (s32[104,1024]{1,0:T(8,128)S(1)}, s32[104,1024]{1,0:T(8,128)S(1)}, u32[]{:S(2)}, u32[]{:S(2)}) collective-permute-start(s32[104,1024]{1,0:T(8,128)S(1)} %combine.7), channel_id=1, source_target_pairs={{0,24},{1,97},{2,26},{3,99},{4,28},{5,101},{6,30},{7,103},{8,0},{9... | collective-permute-start | bytes 1277960 | tf_op jit(solution)/shard_map/ppermute | solution.py:330
  86.0 2.7 %copy-start.1 = (s32[32]{0:T(128)S(1)}, s32[32]{0:T(128)}, u32[]{:S(2)}) copy-start(s32[32]{0:T(128)} %param.5) | copy-start | bytes 388
  86.0 9.8 %collective-permute-start.4 = (s32[104,1024]{1,0:T(8,128)S(1)}, s32[104,1024]{1,0:T(8,128)S(1)}, u32[]{:S(2)}, u32[]{:S(2)}) collective-permute-start(s32[104,1024]{1,0:T(8,128)S(1)} %combine.6), channel_id=1, source_target_pairs={{0,16},{1,65},{2,18},{3,67},{4,20},{5,69},{6,22},{7,71},{8,24},{9,... | collective-permute-start | bytes 1277960 | tf_op jit(solution)/shard_map/ppermute | solution.py:330
  87.7 12.6 %collective-permute-start.3 = (s32[104,1024]{1,0:T(8,128)S(1)}, s32[104,1024]{1,0:T(8,128)S(1)}, u32[]{:S(2)}, u32[]{:S(2)}) collective-permute-start(s32[104,1024]{1,0:T(8,128)S(1)} %combine.5), channel_id=1, source_target_pairs={{0,8},{1,33},{2,10},{3,35},{4,12},{5,37},{6,14},{7,39},{8,16},{9,4... | collective-permute-start | bytes 1277960 | tf_op jit(solution)/shard_map/ppermute | solution.py:330

commit v3 on v2

v3 whole, which is shorter than its diff:
```python
import functools

import jax
import jax.numpy as jnp
from jax import lax
from jax.experimental import pallas as pl
from jax.experimental.pallas import tpu as pltpu
from jax.sharding import PartitionSpec as P


LAGS = 2001
WIDTH = 2048
WORDS = WIDTH // 2
OWNED = 32
DAYS = 4
SIDE = 4
QUANTITIES = 3
TOP = 32766.0
KERNEL_SUM = 6.0
MB = 1 << 20


def params(**settings):
    return pltpu.CompilerParams(**{"vmem_limit_bytes": 32 * MB, **settings})


def encode(value, scale):
    root = value * lax.rsqrt(jnp.abs(value) + 1e-36)
    return (root * scale + 32768.5).astype(jnp.int32)


def pack(low, high):
    return low | (high << 16)


def unpack(word):
    low = (word & 0xFFFF).astype(jnp.float32) - 32768.0
    high = (lax.shift_right_logical(word, 16)).astype(jnp.float32) - 32768.0
    return low * jnp.abs(low), high * jnp.abs(high)


def unit(exponent):
    return jnp.exp2(exponent.astype(jnp.float32)) * (1.0 / (TOP * TOP))


def first_shifts():
    row = lax.broadcasted_iota(jnp.int32, (8, 2 * WIDTH), 0)
    col = lax.broadcasted_iota(jnp.int32, (8, 2 * WIDTH), 1)
    offset = (col - row - WIDTH + 2 * LAGS) % LAGS
    offset = jnp.where(offset > LAGS // 2, offset - LAGS, offset)
    angle = jnp.pi * offset.astype(jnp.float32) / LAGS
    parity = 1.0 - 2.0 * (offset % 2).astype(jnp.float32)
    sine = jnp.where(offset == 0, 1.0, jnp.sin(angle))
    values = jnp.where(offset == 0, 0.0, (jnp.cos(angle) - parity) / (LAGS * sine))
    return values.astype(jnp.bfloat16).astype(jnp.float32)


def fill_table(shifts_ref, table_ref, rolled_ref):
    for q in range(16):
        first = pltpu.roll(shifts_ref[...], 16 * q, 1)
        second = pltpu.roll(shifts_ref[...], 16 * q + 8, 1)
        rolled_ref[16 * q : 16 * q + 16, :] = jnp.concatenate([first, second], 0).astype(jnp.bfloat16)
    for q in range(8):
        for n in range(8):
            for h in range(2):
                start = 128 * (n + 8 * h) - 256 * q + WIDTH
                table_ref[n, 256 * q : 256 * q + 256, 128 * h : 128 * h + 128] = rolled_ref[:, start : start + 128]


TILES = WIDTH // 128
GROUPS = 16


def position(owner, place):
    x, y, core = place >> 3, (place >> 1) & 3, place & 1
    along_x, along_y = (owner // SIDE - x) & 3, (owner % SIDE - y) & 3
    return jnp.where(core == 0, along_x * SIDE + along_y, along_y * SIDE + along_x)


def energy_kernel(place_ref, input_ref, mask_ref, shifts_ref, held_ref, stats_ref, peak_ref, sems):
    last = (LAGS - 128 * (TILES - 1)) * GROUPS

    def fetch(j, size):
        return pltpu.make_async_copy(
            input_ref.at[pl.ds(j * 128 * GROUPS, size), :], held_ref.at[j, pl.ds(0, size), :], sems.at[j]
        )

    for j in range(TILES):
        fetch(j, 128 * GROUPS if j < TILES - 1 else last).start()
    held_ref[TILES - 1, last:, :] = jnp.zeros((128 * GROUPS - last, 128), jnp.bfloat16)
    used = jnp.concatenate([mask_ref[:, 128 * t : 128 * t + 128] for t in range(4)], 0).astype(jnp.float32)

    def tile(j, carry):
        total, most = carry
        for b in range(8):
            values = held_ref[j, 256 * b : 256 * b + 256, :].astype(jnp.float32)
            squares = (values * values).reshape(16, GROUPS, 128)
            total += jnp.sum(squares, axis=0)
            most = jnp.maximum(most, jnp.max(squares, axis=0))
        return total, most

    def step(j, carry):
        fetch(j, 128 * GROUPS).wait()
        return tile(j, carry)

    zero = jnp.zeros((GROUPS, 128), jnp.float32)
    carry = lax.fori_loop(0, TILES - 1, step, (zero, zero))
    fetch(TILES - 1, last).wait()
    total, most = tile(TILES - 1, carry)
    total, most = total * used, most * used

    row = lax.broadcasted_iota(jnp.int32, (8, 128), 0)
    day = lax.broadcasted_iota(jnp.int32, (GROUPS, 128), 0) % DAYS
    stats = peaks = jnp.zeros((8, 128), jnp.float32)
    for d in range(DAYS):
        stats = jnp.where(row == d, jnp.sum(jnp.where(day == d, total, 0.0)), stats)
        stats = jnp.where(row == DAYS + d, jnp.sum(jnp.where(day == d, used, 0.0)), stats)
        peaks = jnp.where(row == d, jnp.max(jnp.where(day == d, most, 0.0)), peaks)
    peak_ref[...] = peaks
    stats_ref[...] = stats


def energies(place, correlations, mask, shifts):
    stored = correlations.reshape(DAYS, 4, 128, LAGS).transpose(3, 1, 0, 2).reshape(LAGS * GROUPS, 128)
    vmem = pl.BlockSpec(memory_space=pltpu.VMEM)
    return pl.pallas_call(
        energy_kernel,
        in_specs=[pl.BlockSpec(memory_space=pltpu.SMEM), pl.BlockSpec(memory_space=pltpu.HBM), vmem, vmem],
        out_specs=[vmem] * 3,
        out_shape=[
            jax.ShapeDtypeStruct((TILES, 128 * GROUPS, 128), jnp.bfloat16),
            jax.ShapeDtypeStruct((8, 128), jnp.float32),
            jax.ShapeDtypeStruct((8, 128), jnp.float32),
        ],
        scratch_shapes=[pltpu.SemaphoreType.DMA((TILES,))],
        compiler_params=params(vmem_limit_bytes=12 * MB),
        name="energy",
    )(place, pltpu.with_memory_space_constraint(stored, pltpu.HBM), mask, shifts)


def rows_kernel(first_tile, last_tile, place_ref, held_ref, mask_ref, *refs):
    out_ref = refs[-1]
    place = place_ref[0]
    row = lax.broadcasted_iota(jnp.int32, (256, 256), 0)
    col = lax.broadcasted_iota(jnp.int32, (256, 256), 1)
    select = ((row // 16 == col % 16) & (row % 16 == col // 16)).astype(jnp.float32).astype(jnp.bfloat16)
    places = [position(owner, place) for owner in range(SIDE * SIDE)]

    def tile(j, carry):
        parts = []
        for b in range(4):
            first = held_ref[j, 512 * b : 512 * b + 256, :]
            second = held_ref[j, 512 * b + 256 : 512 * b + 512, :]
            parts.append(
                jnp.dot(select, jnp.concatenate([first, second], 1), preferred_element_type=jnp.float32)
            )
        for t in range(4):
            for d in range(DAYS):
                at = 16 * (t * DAYS + d)
                pieces = [p[at : at + 16, 128 * h : 128 * h + 128] for p in parts for h in range(2)]
                used = mask_ref[d : d + 1, 128 * t : 128 * t + 128].astype(jnp.float32)
                turned = (jnp.concatenate(pieces, 0) * used).astype(jnp.bfloat16).T
                for i in range(4):
                    lanes = pl.ds(pl.multiple_of(j * 128, 128), 128)
                    out_ref[places[t * 4 + i], d, :, lanes] = turned[OWNED * i : OWNED * i + OWNED, :]
        return carry

    lax.fori_loop(first_tile, last_tile, tile, 0)


def ordered_rows(place, held, mask, before=None):
    vmem = pl.BlockSpec(memory_space=pltpu.VMEM)
    tiles = (0, TILES // 2) if before is None else (TILES // 2, TILES)
    started = [] if before is None else [before]
    return pl.pallas_call(
        functools.partial(rows_kernel, *tiles),
        in_specs=[pl.BlockSpec(memory_space=pltpu.SMEM)] + [vmem] * (2 + len(started)),
        out_specs=vmem,
        out_shape=jax.ShapeDtypeStruct((SIDE * SIDE, DAYS, OWNED, WIDTH), jnp.bfloat16),
        input_output_aliases={3: 0} if started else {},
        compiler_params=params(vmem_limit_bytes=12 * MB),
        cost_estimate=pl.CostEstimate(flops=4 * 10**9, bytes_accessed=8 * MB, transcendentals=0),
        name="rows",
    )(place, held, mask, *started)


def kernel_table(shifts):
    vmem = pl.BlockSpec(memory_space=pltpu.VMEM)
    return pl.pallas_call(
        fill_table,
        in_specs=[vmem],
        out_specs=vmem,
        out_shape=jax.ShapeDtypeStruct((8, WIDTH, 256), jnp.bfloat16),
        scratch_shapes=[pltpu.VMEM((256, 2 * WIDTH), jnp.bfloat16)],
        compiler_params=params(vmem_limit_bytes=12 * MB),
        cost_estimate=pl.CostEstimate(flops=10**9, bytes_accessed=8 * MB, transcendentals=0),
        name="table",
    )(shifts)


def add_kernel(a_ref, b_ref, out_ref):
    out_ref[...] = a_ref[...] + b_ref[...]


def add(a, b):
    vmem = pl.BlockSpec(memory_space=pltpu.VMEM)
    return pl.pallas_call(
        add_kernel,
        in_specs=[vmem] * 2,
        out_specs=vmem,
        out_shape=jax.ShapeDtypeStruct(a.shape, a.dtype),
        compiler_params=params(vmem_limit_bytes=MB),
        name="add",
    )(a, b)


def terms_kernel(k, rows_ref, table_ref, stats_ref, others_ref, peak_ref, out_ref, even_ref, odd_ref):
    total = stats_ref[...] + others_ref[...]
    energy, used = total[:DAYS, :], total[DAYS:, :]
    weight = lax.rsqrt(energy / (LAGS * jnp.maximum(used, 1.0)) + 0.1)
    reach = weight * jnp.sqrt(peak_ref[:DAYS, :])
    bounds = [
        jnp.sum(reach, axis=0, keepdims=True),
        jnp.sum(jnp.minimum(1.0, 2.0 * reach), axis=0, keepdims=True),
        jnp.sum(jnp.minimum(1.0, 2.0 * KERNEL_SUM * reach), axis=0, keepdims=True),
    ]
    powers = [jnp.ceil(jnp.log(jnp.maximum(v, 1e-30) * 1.001) * 1.4426951) for v in bounds]
    scale = [TOP * jnp.exp2(-0.5 * p) for p in powers]
    row = lax.broadcasted_iota(jnp.int32, (8, 128), 0)
    exponents = jnp.where(row == 0, powers[0], jnp.where(row == 1, powers[1], powers[2])).astype(jnp.int32)
    for n in range(WORDS // 128):
        out_ref[SIDE * QUANTITIES * OWNED :, 128 * n : 128 * n + 128] = exponents
    weights = [weight[d : d + 1, :] for d in range(DAYS)]

    def product(n, to_ref):
        to_ref[...] = jnp.dot(rows_ref[k], table_ref[n], preferred_element_type=jnp.float32)

    def finish_block(n, hilbert_ref):
        for l in range(SIDE):
            codes = []
            for h in range(2):
                lanes = pl.ds(pl.multiple_of(n * 128 + h * WORDS, 128), 128)
                linear = real = imag = None
                for d in range(DAYS):
                    at = (l * DAYS + d) * OWNED
                    real_part = rows_ref[k, at : at + OWNED, lanes].astype(jnp.float32) * weights[d]
                    imag_part = hilbert_ref[at : at + OWNED, 128 * h : 128 * h + 128] * weights[d]
                    inverse = lax.rsqrt(real_part * real_part + imag_part * imag_part + 0.25)
                    a, b = real_part * inverse, imag_part * inverse
                    linear = real_part if d == 0 else linear + real_part
                    real = a if d == 0 else real + a
                    imag = b if d == 0 else imag + b
                codes.append([encode(v, scale[q]) for q, v in enumerate((linear, real, imag))])
            for q in range(QUANTITIES):
                at = (l * QUANTITIES + q) * OWNED
                out_ref[at : at + OWNED, pl.ds(pl.multiple_of(n * 128, 128), 128)] = pack(codes[0][q], codes[1][q])

    def step(i, carry):
        product(2 * i + 1, odd_ref)
        finish_block(2 * i, even_ref)
        product(2 * i + 2, even_ref)
        finish_block(2 * i + 1, odd_ref)
        return carry

    product(0, even_ref)
    lax.fori_loop(0, 3, step, 0)
    product(7, odd_ref)
    finish_block(6, even_ref)
    finish_block(7, odd_ref)


def terms(k, rows, table, *stats):
    count = SIDE * QUANTITIES * OWNED + 8
    vmem = pl.BlockSpec(memory_space=pltpu.VMEM)
    return pl.pallas_call(
        functools.partial(terms_kernel, k),
        in_specs=[vmem] * 5,
        out_specs=vmem,
        out_shape=jax.ShapeDtypeStruct((count, WORDS), jnp.int32),
        scratch_shapes=[pltpu.VMEM((SIDE * DAYS * OWNED, 256), jnp.float32)] * 2,
        compiler_params=params(vmem_limit_bytes=24 * MB),
        cost_estimate=pl.CostEstimate(
            flops=2 * SIDE * DAYS * OWNED * WIDTH * WIDTH, bytes_accessed=12 * MB, transcendentals=0
        ),
        name="terms",
    )(rows, table, *stats)


def decode(message_ref, at, exponent, cols):
    k = unit(exponent)
    low, high = unpack(message_ref[at : at + OWNED, cols])
    return low * k, high * k


def gather_kernel(parts, blocks, *refs):
    messages, (out_ref, top_ref) = refs[:parts], refs[parts:]
    rows = blocks * QUANTITIES * OWNED
    top = messages[0][rows : rows + 8, :128]
    for message in messages[1:]:
        top = jnp.maximum(top, message[rows : rows + 8, :128])
    top_ref[...] = top
    for l in range(blocks):
        for j in range(WORDS // 128):
            cols = slice(128 * j, 128 * j + 128)
            for q in range(QUANTITIES):
                at = (l * QUANTITIES + q) * OWNED
                low = high = None
                for message in messages:
                    a, b = decode(message, at, message[rows + q : rows + q + 1, :128], cols)
                    low = a if low is None else low + a
                    high = b if high is None else high + b
                out_ref[at : at + OWNED, cols] = low
                out_ref[at : at + OWNED, 128 * j + WORDS : 128 * j + WORDS + 128] = high


def gather(messages, blocks):
    vmem = pl.BlockSpec(memory_space=pltpu.VMEM)
    return pl.pallas_call(
        functools.partial(gather_kernel, len(messages), blocks),
        in_specs=[vmem] * len(messages),
        out_specs=[vmem] * 2,
        out_shape=[
            jax.ShapeDtypeStruct((blocks * QUANTITIES * OWNED, WIDTH), jnp.float32),
            jax.ShapeDtypeStruct((8, 128), jnp.int32),
        ],
        compiler_params=params(vmem_limit_bytes=16 * MB),
        cost_estimate=pl.CostEstimate(flops=blocks * MB, bytes_accessed=2 * MB, transcendentals=0),
        name="gather",
    )(*messages)


def combine_kernel(l, sums_ref, top_ref, *refs):
    messages, out_ref = refs[:-1], refs[-1]
    rows = SIDE * QUANTITIES * OWNED
    exponents = [message[rows : rows + 8, :128] for message in messages]
    top = top_ref[...]
    for exponent in exponents:
        top = jnp.maximum(top, exponent)
    top = top + 2
    scale = jnp.exp2(-0.5 * top.astype(jnp.float32)) * TOP
    for j in range(WORDS // 128):
        cols = slice(128 * j, 128 * j + 128)
        for q in range(QUANTITIES):
            at = (l * QUANTITIES + q) * OWNED
            low = sums_ref[at : at + OWNED, cols]
            high = sums_ref[at : at + OWNED, 128 * j + WORDS : 128 * j + WORDS + 128]
            for message, exponent in zip(messages, exponents):
                a, b = decode(message, at, exponent[q : q + 1, :], cols)
                low, high = low + a, high + b
            s = scale[q : q + 1, :]
            out_ref[q * OWNED : (q + 1) * OWNED, cols] = pack(encode(low, s), encode(high, s))
        out_ref[QUANTITIES * OWNED :, cols] = top


def combine(l, sums, top, messages):
    vmem = pl.BlockSpec(memory_space=pltpu.VMEM)
    return pl.pallas_call(
        functools.partial(combine_kernel, l),
        in_specs=[vmem] * (2 + len(messages)),
        out_specs=vmem,
        out_shape=jax.ShapeDtypeStruct((QUANTITIES * OWNED + 8, WORDS), jnp.int32),
        compiler_params=params(vmem_limit_bytes=16 * MB),
        cost_estimate=pl.CostEstimate(flops=2 * MB, bytes_accessed=2 * MB, transcendentals=0),
        name="combine",
    )(sums, top, *messages)


def finish_kernel(divisor_ref, sums_ref, message_ref, weighted_ref, linear_ref):
    inverse = 1.0 / divisor_ref[...]
    rows = QUANTITIES * OWNED
    exponents = message_ref[rows : rows + 8, :128]
    for j in range(WORDS // 128):
        cols = slice(128 * j, 128 * j + 128)
        pairs = [decode(message_ref, q * OWNED, exponents[q : q + 1, :], cols) for q in range(QUANTITIES)]
        for h in range(2):
            start = 128 * j + WORDS * h
            size = min(128, LAGS - start)
            linear, real, imag = [
                pairs[q][h] + sums_ref[q * OWNED : (q + 1) * OWNED, start : start + 128] for q in range(QUANTITIES)
            ]
            linear, real, imag = linear * inverse, real * inverse, imag * inverse
            weighted = linear * (real * real + imag * imag)
            linear_ref[:, start : start + size] = linear[:, :size]
            weighted_ref[:, start : start + size] = weighted[:, :size]


def finish(divisor, sums, message):
    vmem = pl.BlockSpec(memory_space=pltpu.VMEM)
    return pl.pallas_call(
        finish_kernel,
        in_specs=[vmem] * 3,
        out_specs=[vmem] * 2,
        out_shape=[jax.ShapeDtypeStruct((OWNED, LAGS), jnp.float32)] * 2,
        compiler_params=params(vmem_limit_bytes=16 * MB),
        name="finish",
    )(divisor, sums, message)


def shift(message, step, first):
    moves = []
    for x in range(SIDE):
        for y in range(SIDE):
            for pair in range(8):
                along_x = (pair % 2 == 0) == first
                to_x = (x + step) % SIDE if along_x else x
                to_y = y if along_x else (y + step) % SIDE
                moves.append(((x * SIDE + y) * 8 + pair, (to_x * SIDE + to_y) * 8 + pair))
    return lax.ppermute(message, ("day", "pair"), moves)


def trade(values, bit):
    moves = [(d * 8 + p, d * 8 + (p ^ bit)) for d in range(SIDE * SIDE) for p in range(8)]
    return lax.ppermute(values, ("day", "pair"), moves)


def stacks(correlations, mask, counts):
    place = (lax.axis_index("day") * 2 + lax.axis_index("pair") % 2).reshape(1)
    shifts = first_shifts()
    held, stats, peak = energies(place, correlations, mask, shifts)
    others = trade(stats, 1)
    table = kernel_table(shifts)
    stats = add(stats, others)
    others = trade(stats, 2)
    rows = ordered_rows(place, held, mask)
    stats = add(stats, others)
    others = trade(stats, 4)
    rows = ordered_rows(place, held, mask, rows)
    rows = rows.reshape(SIDE, SIDE * DAYS * OWNED, WIDTH)

    def wide_step(k):
        piece = terms(k, rows, table, stats, others, peak)
        return shift(piece, k, True) if k else piece

    def narrow_step(l):
        piece = combine(l, sums, top, [ahead, behind])
        return shift(piece, l, False) if l else piece

    far, ahead, behind, own = [wide_step(k) for k in (2, 1, 3, 0)]
    sums, top = gather([own, far], SIDE)
    last, near, far, own = [narrow_step(l) for l in (2, 1, 3, 0)]
    sums, top = gather([own, near, far], 1)
    divisor = jnp.broadcast_to(jnp.maximum(counts.astype(jnp.float32), 1.0)[:, None], (OWNED, 128))
    return tuple(finish(divisor, sums, last))


def solution(mesh):
    placed = (P("day", "pair", None), P("day", "pair"), P(("pair", "day")))
    return jax.shard_map(
        stacks,
        mesh=mesh,
        in_specs=placed,
        out_specs=(P(("pair", "day"), None), P(("pair", "day"), None)),
        check_vma=False,
    )
```

time: 102 us -> 98.8 us (0.969)
  blocking collectives: 10.7 us -> 0 us
  starting transfers between devices: 9.65 us -> 16.1 us
  Pallas kernels: 45.7 us -> 48.3 us
  waiting for transfers between devices: 33.7 us -> 32 us
    all_to_all x1 -> x0, blocking collectives: 10.7 us -> none  [stacks(): stats = lax.all_to_all(stats, 'pair', 0, 0, tiled=True)]
    ppermute x0 -> x3, starting transfers between devices: none -> 5.84 us  [trade(): return lax.ppermute(values, ('day', 'pair'), moves)]
    pallas_call x10 -> x17, Pallas kernels: 45.7 us -> 48.3 us  [the longest x4 29.6 us: terms(): pl.pallas_call(functools.partial(terms_kernel, k), in_specs=[vmem] * 5, o...]
    ppermute x6, waiting for transfers between devices: 33.7 us -> 32 us  [shift(): return lax.ppermute(message, ('day', 'pair'), moves)]
  transfers between devices with their start and end apart: 6 -> 9, of which waited for: 5 -> 5; matrix products, arithmetic and copies ran while one was open for 0% -> 0% of each run, Pallas kernels for 24% -> 36%
where the time goes in v3:
time: 98.8 us; the launch traced here: 98.7 us
  Pallas kernels  48.3 us (49%)
  waiting for transfers between devices  32 us (32%)
  starting transfers between devices  16.1 us (16%)
    ppermute x6, waiting for transfers between devices, shift(): return lax.ppermute(message, ('day', 'pair'), moves)  32 us
    pallas_call x4, Pallas kernels, terms(): pl.pallas_call(functools.partial(terms_kernel, k), in_specs=[vmem] * 5, o...  29.6 us
    ppermute x6, starting transfers between devices, shift(): return lax.ppermute(message, ('day', 'pair'), moves)  10.3 us
    pallas_call x2, Pallas kernels, ordered_rows(): pl.pallas_call(functools.partial(rows_kernel, *tiles), in_specs=[pl.Block...  7.63 us
    ppermute x3, starting transfers between devices, trade(): return lax.ppermute(values, ('day', 'pair'), moves)  5.84 us
    pallas_call x1, Pallas kernels, energies(): pl.pallas_call(energy_kernel, in_specs=[pl.BlockSpec(memory_space=pltpu.S...  3.76 us
    pallas_call x4, Pallas kernels, combine(): pl.pallas_call(functools.partial(combine_kernel, l), in_specs=[vmem] * (2...  2.4 us
  transfers between devices with their start and end apart: 9, of which 5 were waited for; matrix products, arithmetic and copies ran while one was open for 0% of the time, Pallas kernels for 36%

profile of v3, /device:TPU:0, one launch (start us, length us, event | category | flops | bytes accessed | tf_op | source)
XLA Modules:
  0.0 98.7 jit_solution(17525303666740204054)
XLA Ops:
  0.6 0.6 fusion.12.shifts_ref
  1.3 0.7 copy-done
  2.0 3.8 %energy.1 = (bf16[16,2048,128]{2,1,0:T(8,128)(2,1)S(1)}, f32[8,128]{1,0:T(8,128)S(1)}, f32[8,128]{1,0:T(8,128)S(1)}) custom-call(s32[1]{0:T(128)} %bitcast.place_ref, bf16[32016,128]{1,0:T(8,128)(2,1)} %bitcast.11, s32[4,512]{1,0:T(4,128)S(1)} %copy-done, f32[8,4096]{1,0:T(8,128)S(1)} %fusion.12.shifts_ref), custom_call_target="tpu_custom_call" | custom-call | tf_op jit(solution)/shard_map/energy/pallas_call | solution.py:126
  5.9 3.8 %rows.2.refs_0_ = bf16[16,4,32,2048]{3,2,1,0:T(8,128)(2,1)S(1)} custom-call(s32[1]{0:T(128)} %bitcast.place_ref, bf16[16,2048,128]{2,1,0:T(8,128)(2,1)S(1)} %get-tuple-element.8.held_ref, s32[4,512]{1,0:T(4,128)S(1)} %copy-done), custom_call_target="tpu_custom_call" | custom-call | flops 4000000000 | bytes 8388608 | tf_op jit(solution)/shard_map/rows/pallas_call | solution.py:175
  9.7 2.1 %collective-permute-start.1 = (f32[8,128]{1,0:T(8,128)S(1)}, f32[8,128]{1,0:T(8,128)S(1)}, u32[]{:S(2)}, u32[]{:S(2)}) collective-permute-start(f32[8,128]{1,0:T(8,128)S(1)} %add.83.a_ref), channel_id=1, source_target_pairs={{0,2},{1,3},{2,0},{3,1},{4,6},{5,7},{6,4},{7,5},{8,10},{9,11},{10,... | collective-permute-start | bytes 12296 | tf_op jit(solution)/shard_map/ppermute | solution.py:413
  11.8 3.8 %rows.3 = bf16[16,4,32,2048]{3,2,1,0:T(8,128)(2,1)S(1)} custom-call(s32[1]{0:T(128)} %bitcast.place_ref, bf16[16,2048,128]{2,1,0:T(8,128)(2,1)S(1)} %get-tuple-element.8.held_ref, s32[4,512]{1,0:T(4,128)S(1)} %copy-done, bf16[16,4,32,2048]{3,2,1,0:T(8,128)(2,1)S(1)} %rows.2.refs_0_), custom_call_target="tpu_custom_call", output_to_operand_aliasing={{}: (3, {})} | custom-call | flops 4000000000 | bytes 8388608 | tf_op jit(solution)/shard_map/rows/pallas_call | solution.py:175
  15.6 3.7 %collective-permute-start.2 = (f32[8,128]{1,0:T(8,128)S(1)}, f32[8,128]{1,0:T(8,128)S(1)}, u32[]{:S(2)}, u32[]{:S(2)}) collective-permute-start(f32[8,128]{1,0:T(8,128)S(1)} %add.84.stats_ref), channel_id=1, source_target_pairs={{0,4},{1,5},{2,6},{3,7},{4,0},{5,1},{6,2},{7,3},{8,12},{9,13},{10,... | collective-permute-start | bytes 12296 | tf_op jit(solution)/shard_map/ppermute | solution.py:413
  19.3 2.0 %table.1.table_ref = bf16[8,2048,256]{2,1,0:T(8,128)(2,1)S(1)} custom-call(f32[8,4096]{1,0:T(8,128)S(1)} %fusion.12.shifts_ref), custom_call_target="tpu_custom_call" | custom-call | flops 1000000000 | bytes 8388608 | tf_op jit(solution)/shard_map/table/pallas_call | solution.py:189
  21.3 7.4 %terms.7 = s32[392,1024]{1,0:T(8,128)S(1)} custom-call(bf16[4,512,2048]{2,1,0:T(8,128)(2,1)S(1)} %bitcast.7, bf16[8,2048,256]{2,1,0:T(8,128)(2,1)S(1)} %table.1.table_ref, f32[8,128]{1,0:T(8,128)S(1)} %add.84.stats_ref, f32[8,128]{1,0:T(8,128)S(1)} %collective-permute-done.2.others_ref, f32[8,128]{1,0:T(8,128)S(1)} %get-tuple-element.10.peak_ref), custom_call_target="tpu_custom_call" | custom-call | flops 4294967296 | bytes 12582912 | tf_op jit(solution)/shard_map/terms/pallas_call | solution.py:275
  28.7 2.8 %collective-permute-start.5 = (s32[392,1024]{1,0:T(8,128)S(1)}, s32[392,1024]{1,0:T(8,128)S(1)}, u32[]{:S(2)}, u32[]{:S(2)}) collective-permute-start(s32[392,1024]{1,0:T(8,128)S(1)} %terms.7), channel_id=1, source_target_pairs={{0,96},{1,25},{2,98},{3,27},{4,100},{5,29},{6,102},{7,31},{8,104},... | collective-permute-start | bytes 4816904 | tf_op jit(solution)/shard_map/ppermute | solution.py:408
  31.5 7.4 %terms.5 = s32[392,1024]{1,0:T(8,128)S(1)} custom-call(bf16[4,512,2048]{2,1,0:T(8,128)(2,1)S(1)} %bitcast.8, bf16[8,2048,256]{2,1,0:T(8,128)(2,1)S(1)} %table.1.table_ref, f32[8,128]{1,0:T(8,128)S(1)} %add.84.stats_ref, f32[8,128]{1,0:T(8,128)S(1)} %collective-permute-done.2.others_ref, f32[8,128]{1,0:T(8,128)S(1)} %get-tuple-element.10.peak_ref), custom_call_target="tpu_custom_call" | custom-call | flops 4294967296 | bytes 12582912 | tf_op jit(solution)/shard_map/terms/pallas_call | solution.py:275
  38.9 1.1 %collective-permute-start.3 = (s32[392,1024]{1,0:T(8,128)S(1)}, s32[392,1024]{1,0:T(8,128)S(1)}, u32[]{:S(2)}, u32[]{:S(2)}) collective-permute-start(s32[392,1024]{1,0:T(8,128)S(1)} %terms.5), channel_id=1, source_target_pairs={{0,64},{1,17},{2,66},{3,19},{4,68},{5,21},{6,70},{7,23},{8,72},{9,... | collective-permute-start | bytes 4816904 | tf_op jit(solution)/shard_map/ppermute | solution.py:408
  40.0 7.4 %terms.6 = s32[392,1024]{1,0:T(8,128)S(1)} custom-call(bf16[4,512,2048]{2,1,0:T(8,128)(2,1)S(1)} %bitcast.9, bf16[8,2048,256]{2,1,0:T(8,128)(2,1)S(1)} %table.1.table_ref, f32[8,128]{1,0:T(8,128)S(1)} %add.84.stats_ref, f32[8,128]{1,0:T(8,128)S(1)} %collective-permute-done.2.others_ref, f32[8,128]{1,0:T(8,128)S(1)} %get-tuple-element.10.peak_ref), custom_call_target="tpu_custom_call" | custom-call | flops 4294967296 | bytes 12582912 | tf_op jit(solution)/shard_map/terms/pallas_call | solution.py:275
  47.4 0.9 collective-permute-start.4
  48.3 7.4 %terms.4.refs_0_ = s32[392,1024]{1,0:T(8,128)S(1)} custom-call(bf16[4,512,2048]{2,1,0:T(8,128)(2,1)S(1)} %bitcast.10, bf16[8,2048,256]{2,1,0:T(8,128)(2,1)S(1)} %table.1.table_ref, f32[8,128]{1,0:T(8,128)S(1)} %add.84.stats_ref, f32[8,128]{1,0:T(8,128)S(1)} %collective-permute-done.2.others_ref, f32[8,128]{1,0:T(8,128)S(1)} %get-tuple-element.10.peak_ref), custom_call_target="tpu_custom_call" | custom-call | flops 4294967296 | bytes 12582912 | tf_op jit(solution)/shard_map/terms/pallas_call | solution.py:275
  55.7 5.8 %collective-permute-done.3.refs_1_ = s32[392,1024]{1,0:T(8,128)S(1)} collective-permute-done((s32[392,1024]{1,0:T(8,128)S(1)}, s32[392,1024]{1,0:T(8,128)S(1)}, u32[]{:S(2)}, u32[]{:S(2)}) %collective-permute-start.3) | collective-permute-done | bytes 1605664 | tf_op jit(solution)/shard_map/ppermute | solution.py:408
  61.5 1.4 %gather.2 = (f32[384,2048]{1,0:T(8,128)S(1)}, s32[8,128]{1,0:T(8,128)S(1)}) custom-call(s32[392,1024]{1,0:T(8,128)S(1)} %terms.4.refs_0_, s32[392,1024]{1,0:T(8,128)S(1)} %collective-permute-done.3.refs_1_), custom_call_target="tpu_custom_call" | custom-call | flops 4194304 | bytes 2097152 | tf_op jit(solution)/shard_map/gather/pallas_call | solution.py:318
  62.9 4.1 %collective-permute-done.5.refs_1_ = s32[392,1024]{1,0:T(8,128)S(1)} collective-permute-done((s32[392,1024]{1,0:T(8,128)S(1)}, s32[392,1024]{1,0:T(8,128)S(1)}, u32[]{:S(2)}, u32[]{:S(2)}) %collective-permute-start.5) | collective-permute-done | bytes 1605664 | tf_op jit(solution)/shard_map/ppermute | solution.py:408
  67.0 11.6 %collective-permute-done.4.refs_0_ = s32[392,1024]{1,0:T(8,128)S(1)} collective-permute-done((s32[392,1024]{1,0:T(8,128)S(1)}, s32[392,1024]{1,0:T(8,128)S(1)}, u32[]{:S(2)}, u32[]{:S(2)}) %collective-permute-start.4) | collective-permute-done | bytes 1605664 | tf_op jit(solution)/shard_map/ppermute | solution.py:408
  79.2 3.1 %collective-permute-start.7 = (s32[104,1024]{1,0:T(8,128)S(1)}, s32[104,1024]{1,0:T(8,128)S(1)}, u32[]{:S(2)}, u32[]{:S(2)}) collective-permute-start(s32[104,1024]{1,0:T(8,128)S(1)} %combine.6), channel_id=1, source_target_pairs={{0,24},{1,97},{2,26},{3,99},{4,28},{5,101},{6,30},{7,103},{8,0},{9... | collective-permute-start | bytes 1277960 | tf_op jit(solution)/shard_map/ppermute | solution.py:408
  83.7 2.3 %collective-permute-start.8 = (s32[104,1024]{1,0:T(8,128)S(1)}, s32[104,1024]{1,0:T(8,128)S(1)}, u32[]{:S(2)}, u32[]{:S(2)}) collective-permute-start(s32[104,1024]{1,0:T(8,128)S(1)} %combine.7), channel_id=1, source_target_pairs={{0,16},{1,65},{2,18},{3,67},{4,20},{5,69},{6,22},{7,71},{8,24},{9,... | collective-permute-start | bytes 1277960 | tf_op jit(solution)/shard_map/ppermute | solution.py:408
  86.5 1.5 %collective-permute-done.7.refs_2_ = s32[104,1024]{1,0:T(8,128)S(1)} collective-permute-done((s32[104,1024]{1,0:T(8,128)S(1)}, s32[104,1024]{1,0:T(8,128)S(1)}, u32[]{:S(2)}, u32[]{:S(2)}) %collective-permute-start.7) | collective-permute-done | bytes 426016 | tf_op jit(solution)/shard_map/ppermute | solution.py:408
  88.0 8.9 %collective-permute-done.6.refs_1_ = s32[104,1024]{1,0:T(8,128)S(1)} collective-permute-done((s32[104,1024]{1,0:T(8,128)S(1)}, s32[104,1024]{1,0:T(8,128)S(1)}, u32[]{:S(2)}, u32[]{:S(2)}) %collective-permute-start.6) | collective-permute-done | bytes 426016 | tf_op jit(solution)/shard_map/ppermute | solution.py:408
  97.6 1.0 %finish.1 = (f32[32,2001]{1,0:T(8,128)}, f32[32,2001]{1,0:T(8,128)}) custom-call(f32[32,128]{1,0:T(8,128)S(1)} %broadcast_in_dim.11.divisor_ref, f32[96,2048]{1,0:T(8,128)S(1)} %get-tuple-element.13.sums_ref, s32[104,1024]{1,0:T(8,128)S(1)} %collective-permute-done.8.message_ref), custom_call_target="tpu_custom_call" | custom-call | tf_op jit(solution)/shard_map/finish/pallas_call | solution.py:389
  (18 shorter events, 3.3 us)
Async XLA Ops:
  1.3 0.7 copy-start
  5.8 3.9 %collective-permute-start = (f32[8,128]{1,0:T(8,128)S(1)}, f32[8,128]{1,0:T(8,128)S(1)}, u32[]{:S(2)}, u32[]{:S(2)}) collective-permute-start(f32[8,128]{1,0:T(8,128)S(1)} %get-tuple-element.9.a_ref), channel_id=1, source_target_pairs={{0,1},{1,0},{2,3},{3,2},{4,5},{5,4},{6,7},{7,6},{8,9},{9,8},{10,11... | collective-permute-start | bytes 12296 | tf_op jit(solution)/shard_map/ppermute | solution.py:413
  9.7 5.9 %collective-permute-start.1 = (f32[8,128]{1,0:T(8,128)S(1)}, f32[8,128]{1,0:T(8,128)S(1)}, u32[]{:S(2)}, u32[]{:S(2)}) collective-permute-start(f32[8,128]{1,0:T(8,128)S(1)} %add.83.a_ref), channel_id=1, source_target_pairs={{0,2},{1,3},{2,0},{3,1},{4,6},{5,7},{6,4},{7,5},{8,10},{9,11},{10,... | collective-permute-start | bytes 12296 | tf_op jit(solution)/shard_map/ppermute | solution.py:413
  15.6 5.6 %collective-permute-start.2 = (f32[8,128]{1,0:T(8,128)S(1)}, f32[8,128]{1,0:T(8,128)S(1)}, u32[]{:S(2)}, u32[]{:S(2)}) collective-permute-start(f32[8,128]{1,0:T(8,128)S(1)} %add.84.stats_ref), channel_id=1, source_target_pairs={{0,4},{1,5},{2,6},{3,7},{4,0},{5,1},{6,2},{7,3},{8,12},{9,13},{10,... | collective-permute-start | bytes 12296 | tf_op jit(solution)/shard_map/ppermute | solution.py:413
  28.7 38.4 %collective-permute-start.5 = (s32[392,1024]{1,0:T(8,128)S(1)}, s32[392,1024]{1,0:T(8,128)S(1)}, u32[]{:S(2)}, u32[]{:S(2)}) collective-permute-start(s32[392,1024]{1,0:T(8,128)S(1)} %terms.7), channel_id=1, source_target_pairs={{0,96},{1,25},{2,98},{3,27},{4,100},{5,29},{6,102},{7,31},{8,104},... | collective-permute-start | bytes 4816904 | tf_op jit(solution)/shard_map/ppermute | solution.py:408
  38.9 22.6 %collective-permute-start.3 = (s32[392,1024]{1,0:T(8,128)S(1)}, s32[392,1024]{1,0:T(8,128)S(1)}, u32[]{:S(2)}, u32[]{:S(2)}) collective-permute-start(s32[392,1024]{1,0:T(8,128)S(1)} %terms.5), channel_id=1, source_target_pairs={{0,64},{1,17},{2,66},{3,19},{4,68},{5,21},{6,70},{7,23},{8,72},{9,... | collective-permute-start | bytes 4816904 | tf_op jit(solution)/shard_map/ppermute | solution.py:408
  47.4 31.3 %collective-permute-start.4 = (s32[392,1024]{1,0:T(8,128)S(1)}, s32[392,1024]{1,0:T(8,128)S(1)}, u32[]{:S(2)}, u32[]{:S(2)}) collective-permute-start(s32[392,1024]{1,0:T(8,128)S(1)} %terms.6), channel_id=1, source_target_pairs={{0,32},{1,9},{2,34},{3,11},{4,36},{5,13},{6,38},{7,15},{8,40},{9,1... | collective-permute-start | bytes 4816904 | tf_op jit(solution)/shard_map/ppermute | solution.py:408
  79.2 8.8 %collective-permute-start.7 = (s32[104,1024]{1,0:T(8,128)S(1)}, s32[104,1024]{1,0:T(8,128)S(1)}, u32[]{:S(2)}, u32[]{:S(2)}) collective-permute-start(s32[104,1024]{1,0:T(8,128)S(1)} %combine.6), channel_id=1, source_target_pairs={{0,24},{1,97},{2,26},{3,99},{4,28},{5,101},{6,30},{7,103},{8,0},{9... | collective-permute-start | bytes 1277960 | tf_op jit(solution)/shard_map/ppermute | solution.py:408
  83.0 3.0 %copy-start.1 = (s32[32]{0:T(128)S(1)}, s32[32]{0:T(128)}, u32[]{:S(2)}) copy-start(s32[32]{0:T(128)} %param.5) | copy-start | bytes 388
  83.0 14.0 %collective-permute-start.6 = (s32[104,1024]{1,0:T(8,128)S(1)}, s32[104,1024]{1,0:T(8,128)S(1)}, u32[]{:S(2)}, u32[]{:S(2)}) collective-permute-start(s32[104,1024]{1,0:T(8,128)S(1)} %combine.5), channel_id=1, source_target_pairs={{0,8},{1,33},{2,10},{3,35},{4,12},{5,37},{6,14},{7,39},{8,16},{9,4... | collective-permute-start | bytes 1277960 | tf_op jit(solution)/shard_map/ppermute | solution.py:408
  83.7 13.9 %collective-permute-start.8 = (s32[104,1024]{1,0:T(8,128)S(1)}, s32[104,1024]{1,0:T(8,128)S(1)}, u32[]{:S(2)}, u32[]{:S(2)}) collective-permute-start(s32[104,1024]{1,0:T(8,128)S(1)} %combine.7), channel_id=1, source_target_pairs={{0,16},{1,65},{2,18},{3,67},{4,20},{5,69},{6,22},{7,71},{8,24},{9,... | collective-permute-start | bytes 1277960 | tf_op jit(solution)/shard_map/ppermute | solution.py:408
